TPU v7x, 256 devices: a 4x2x16 block of a 4x16x16 slice. The times are simulated.
256 devices in a mesh: groups: 2 (over y), nodes: 128 (over z, x, core).
Axes of the slice: x: 4, y: 2, z: 16, core: 2. Of those that a mesh axis runs over, the one named last changes fastest.
The devices are a block of a 4x16x16 slice.
Arguments:
- grid: bfloat16 [32768, 512], P(('groups', 'nodes')), parts along dimension 0, may hold values from -6 to 6
- hidden: bfloat16 [65536, 512], P(('groups', 'nodes')), parts along dimension 0, may hold values from -6 to 6
- enc_nbr: int32 [32768, 32], P('nodes'), may hold values from 0 to 16383, as said below
- dec_nbr: int32 [16384, 3], P('nodes'), may hold values from 0 to 32767, as said below
- enc_qkv: bfloat16 [512, 1536], replicated, may hold values from -0.25 to 0.25
- enc_out: bfloat16 [512, 512], replicated, may hold values from -0.25 to 0.25
- proc_qkv: bfloat16 [512, 1536], replicated, may hold values from -0.25 to 0.25
- proc_out: bfloat16 [512, 512], replicated, may hold values from -0.25 to 0.25
- dec_qkv: bfloat16 [512, 1536], replicated, may hold values from -0.25 to 0.25
- dec_out: bfloat16 [512, 512], replicated, may hold values from -0.25 to 0.25
- mlp_in: bfloat16 [512, 2048], replicated, may hold values from -0.25 to 0.25
- mlp_out: bfloat16 [2048, 512], replicated, may hold values from -0.125 to 0.125
Outputs:
- grid_out: bfloat16 [32768, 512], P(('groups', 'nodes')), parts along dimension 0
- hidden_two: bfloat16 [65536, 512], P(('groups', 'nodes')), parts along dimension 0
There are 2 independent parts, one for each index of `groups`. A program takes and returns all parts, laid end to end along the dimension named above; an argument that names none is the same for every part. Nothing has to cross between parts.
Inputs may be any that keep to these rules, and one draw needn't show every extreme that they name: `enc_nbr`: row i names grid nodes of regions r - 1 to r + 1 only, with r = i // 256, region r holding grid nodes r * 128 to (r + 1) * 128 - 1. `dec_nbr`: row i names hidden nodes of regions r - 1 to r + 1 only, with r = i // 128, region r holding hidden nodes r * 256 to (r + 1) * 256 - 1.
All inputs are finite; a program needn't handle non-finite values.
Results may differ from a plain program's by a relative error of at most 0.015.
Values may be sent and summed in bfloat16 or wider, within the bound.
No kernel may reach another device: no remote copies, remote signals or barrier semaphores. Data moves between devices by JAX's collectives and lax.ppermute only.
A program may use at most 64 MiB of HBM per device.

v0:
```python
import jax
import jax.numpy as jnp
from jax import lax
from jax.sharding import PartitionSpec as P

HEADS = 16


EPSILON = 1e-05


def padded(shard, sides, width):
    for axis, dim in sides:
        devices, length = (lax.axis_size(axis), shard.shape[dim])
        up = [(i, (i + 1) % devices) for i in range(devices - 1)]
        down = [(j, i) for i, j in up]
        last = lax.slice_in_dim(shard, length - width, length, axis=dim)
        leading = lax.slice_in_dim(shard, 0, width, axis=dim)
        before = lax.ppermute(last, axis, up)
        after = lax.ppermute(leading, axis, down)
        shard = jnp.concatenate([before, shard, after], axis=dim)
    return shard


def partner_2(shard, axis, stride):
    return lax.ppermute(shard, axis, [(i, i ^ 1 << stride) for i in range(lax.axis_size(axis))])


def layer_norm(values):
    values = values.astype(jnp.float32)
    center = values - jnp.mean(values, axis=-1, keepdims=True)
    spread = jnp.mean(center * center, axis=-1, keepdims=True)
    return (center * lax.rsqrt(spread + EPSILON)).astype(jnp.bfloat16)


def product(left, right):
    return jnp.dot(left, right, preferred_element_type=jnp.float32)


def list_counts(lists, column_count):
    columns = jnp.arange(column_count, dtype=jnp.int32)
    return jnp.sum((lists[:, :, None] == columns[None, None, :]).astype(jnp.float32), axis=1)


def dense_partial(queries, key_values, counts):
    row_count = queries.shape[0]
    column_count = key_values.shape[0]
    model_width = queries.shape[1]
    head_size = model_width // HEADS
    query_heads = queries.reshape(row_count, HEADS, head_size)
    key_heads = key_values[:, :model_width].reshape(column_count, HEADS, head_size)
    value_heads = (
        key_values[:, model_width:].astype(jnp.float32).reshape(column_count, HEADS, head_size)
    )
    scores = jnp.einsum("nhd,chd->hnc", query_heads, key_heads, preferred_element_type=jnp.float32)
    scores = scores / jnp.sqrt(jnp.float32(head_size))
    present = (counts > 0.0)[None, :, :]
    scores = jnp.where(present, scores, -1e30)
    maxima = jnp.max(scores, axis=-1)
    weights = counts[None, :, :] * jnp.exp(scores - maxima[:, :, None])
    totals = jnp.sum(weights, axis=-1)
    numerator = jnp.einsum("hnc,chd->hnd", weights, value_heads, preferred_element_type=jnp.float32)
    return (maxima, totals, numerator)


def dense_attend(queries, key_values, counts):
    maxima, totals, numerator = dense_partial(queries, key_values, counts)
    mixed = numerator / totals[:, :, None]
    return jnp.transpose(mixed, (1, 0, 2)).reshape(queries.shape)


def window_attend(queries, key_values):
    row_count = queries.shape[0]
    key_count = key_values.shape[0]
    model_width = queries.shape[1]
    head_size = model_width // HEADS
    query_heads = queries.reshape(row_count, HEADS, head_size)
    key_heads = key_values[:, :model_width].reshape(key_count, HEADS, head_size)
    value_heads = (
        key_values[:, model_width:].astype(jnp.float32).reshape(key_count, HEADS, head_size)
    )
    scores = jnp.einsum("nhd,whd->hnw", query_heads, key_heads, preferred_element_type=jnp.float32)
    weights = jax.nn.softmax(scores / jnp.sqrt(jnp.float32(head_size)), axis=-1)
    mixed = jnp.einsum("hnw,whd->hnd", weights, value_heads, preferred_element_type=jnp.float32)
    return jnp.transpose(mixed, (1, 0, 2)).reshape(row_count, model_width)


def local(
    grid,
    hidden,
    enc_nbr,
    dec_nbr,
    enc_qkv,
    enc_out,
    proc_qkv,
    proc_out,
    dec_qkv,
    dec_out,
    mlp_in,
    mlp_out,
):
    model_width = grid.shape[1]
    grid_rows = grid.shape[0]
    hidden_rows = hidden.shape[0]
    device_pos = lax.axis_index("nodes")
    grid_normed = layer_norm(grid)
    enc_queries = product(layer_norm(hidden), enc_qkv[:, :model_width]).astype(jnp.bfloat16)
    padded_normed = padded(grid_normed, (("nodes", 0),), grid_rows)
    padded_pairs = product(padded_normed, enc_qkv[:, model_width:]).astype(jnp.bfloat16)
    local_lists = enc_nbr - (device_pos - 1) * grid_rows
    counts = list_counts(local_lists, 3 * grid_rows)
    enc_mix = dense_attend(enc_queries, padded_pairs, counts).astype(jnp.bfloat16)
    hidden_one = (hidden.astype(jnp.float32) + product(enc_mix, enc_out)).astype(jnp.bfloat16)
    proc_all = product(layer_norm(hidden_one), proc_qkv).astype(jnp.bfloat16)
    window_pairs = proc_all[:, model_width:]
    partner = partner_2(window_pairs, "nodes", 0)
    lower_half = device_pos >> 0 & 1 == 0
    window_pairs = jnp.where(
        lower_half,
        jnp.concatenate([window_pairs, partner], axis=0),
        jnp.concatenate([partner, window_pairs], axis=0),
    )
    proc_mix = window_attend(proc_all[:, :model_width], window_pairs).astype(jnp.bfloat16)
    hidden_two = (hidden_one.astype(jnp.float32) + product(proc_mix, proc_out)).astype(jnp.bfloat16)
    dec_queries = product(grid_normed, dec_qkv[:, :model_width]).astype(jnp.bfloat16)
    padded_state = padded(hidden_two, (("nodes", 0),), hidden_rows)
    padded_hidden = product(layer_norm(padded_state), dec_qkv[:, model_width:]).astype(jnp.bfloat16)
    dec_local = dec_nbr - (device_pos - 1) * hidden_rows
    dec_counts = list_counts(dec_local, 3 * hidden_rows)
    dec_mix = dense_attend(dec_queries, padded_hidden, dec_counts).astype(jnp.bfloat16)
    grid_one = (grid.astype(jnp.float32) + product(dec_mix, dec_out)).astype(jnp.bfloat16)
    mlp_hidden = jax.nn.gelu(product(layer_norm(grid_one), mlp_in)).astype(jnp.bfloat16)
    grid_out = (grid_one.astype(jnp.float32) + product(mlp_hidden, mlp_out)).astype(jnp.bfloat16)
    return (grid_out, hidden_two)


def solution(mesh):
    return jax.shard_map(
        local,
        mesh=mesh,
        in_specs=(
            P(("groups", "nodes"), None),
            P(("groups", "nodes"), None),
            P("nodes", None),
            P("nodes", None),
            P(),
            P(),
            P(),
            P(),
            P(),
            P(),
            P(),
            P(),
        ),
        out_specs=(P(("groups", "nodes"), None), P(("groups", "nodes"), None)),
        check_vma=False,
    )
```

profile of v0, /device:TPU:33, one launch (start us, length us, event | category | flops | bytes accessed | tf_op | source)
XLA Modules:
  0.0 90.1 jit_solution(9380029243227601945)
XLA Ops:
  4.0 22.4 %collective-permute-start.1 = (bf16[128,512]{1,0:T(8,128)(2,1)S(1)}, bf16[128,512]{1,0:T(8,128)(2,1)S(1)}, u32[]{:S(2)}, u32[]{:S(2)}) collective-permute-start(bf16[128,512]{1,0:T(8,128)(2,1)S(1)} %fusion.73), channel_id=1, source_target_pairs={{1,0},{2,1},{3,2},{4,3},{5,4},{6,5},{7,6},{8,7},{9,8},{10,9},{11,1... | collective-permute-start | bytes 393224 | tf_op jit(solution)/shard_map/ppermute | solution.py:20
  26.3 2.0 %collective-permute-start = (bf16[128,512]{1,0:T(8,128)(2,1)S(1)}, bf16[128,512]{1,0:T(8,128)(2,1)S(1)}, u32[]{:S(2)}, u32[]{:S(2)}) collective-permute-start(bf16[128,512]{1,0:T(8,128)(2,1)S(1)} %fusion.73), channel_id=1, source_target_pairs={{0,1},{1,2},{2,3},{3,4},{4,5},{5,6},{6,7},{7,8},{8,9},{9,10},{10,1... | collective-permute-start | bytes 393224 | tf_op jit(solution)/shard_map/ppermute | solution.py:19
  29.1 2.2 %convert_reduce_fusion = f32[256,384]{1,0:T(8,128)S(1)} fusion(s32[256,32]{1,0:T(8,128)S(1)} %copy.37), kind=kLoop, calls=%fused_computation | loop fusion | flops 9338880 | bytes 425984 | tf_op jit(solution)/shard_map/reduce_sum | solution.py:42
  33.6 1.5 %convolution_convert_fusion.3 = bf16[256,512]{1,0:T(8,128)(2,1)S(1)} fusion(bf16[512,1536]{1,0:T(8,128)(2,1)} %param.16, bf16[256,512]{1,0:T(8,128)(2,1)} %param.13, f32[256]{0:T(256)S(1)} %add_rsqrt_fusion.2, f32[256]{0:T(256)S(1)} %broadcast_multiply_fusion.2), kind=kOutput, calls=%fused_computation.46 | convolution fusion | flops 134873088 | bytes 1050624 | tf_op jit(solution)/shard_map/dot_general | solution.py:37
  35.9 1.8 %convolution_convert_fusion.2 = bf16[384,1024]{1,0:T(8,128)(2,1)S(1)} fusion(bf16[512,1536]{1,0:T(8,128)(2,1)} %param.16, bf16[128,512]{1,0:T(8,128)(2,1)S(1)} %collective-permute-done.1, bf16[128,512]{1,0:T(8,128)(2,1)S(1)} %fusion.73, bf16[128,512]{1,0:T(8,128)(2,1)S(1)} %collective-permute-done), kind=kOutput, calls=%fused_computation.39 | convolution fusion | flops 404226048 | bytes 2228224 | tf_op jit(solution)/shard_map/dot_general | solution.py:37
  38.9 2.3 %fusion.3 = (f32[16,256]{1,0:T(8,128)S(1)}, f32[16,256,384]{2,1,0:T(8,128)S(1)}) fusion(pred[256,384]{1,0:T(8,128)(4,1)} %broadcast_compare_fusion, bf16[256,16,32]{0,2,1:T(8,128)(2,1)S(1)} %bitcast.50, bf16[384,16,32]{0,2,1:T(8,128)(2,1)S(1)} %bitcast.49), kind=kOutput, calls=%fused_computation.11 | convolution fusion | flops 105377792 | bytes 7061504 | tf_op jit(solution)/shard_map/nhd,chd->hnc/dot_general | solution.py:55
  41.2 2.1 %fusion.5 = f32[16,256]{1,0:T(8,128)S(1)} fusion(f32[16,256,384]{2,1,0:T(8,128)S(1)} %get-tuple-element.9, f32[16,256]{1,0:T(8,128)S(1)} %get-tuple-element.8, f32[256,384]{1,0:T(8,128)S(1)} %convert_reduce_fusion, pred[256,384]{1,0:T(8,128)(4,1)S(1)} %copy-done.6), kind=kLoop, calls=%fused_computation.13 | loop fusion | flops 7860224 | bytes 6815744 | tf_op jit(solution)/shard_map/reduce_sum | solution.py:61
  43.4 2.1 %fusion.50 = bf16[256,16,32]{0,2,1:T(8,128)(2,1)S(1)} fusion(bf16[384,16,32]{0,2,1:T(8,128)(2,1)S(1)} %bitcast.55, f32[16,256,384]{2,1,0:T(8,128)S(1)} %get-tuple-element.9, f32[16,256]{1,0:T(8,128)S(1)} %get-tuple-element.8, f32[256,384]{1,0:T(8,128)S(1)} %convert_reduce_fusion, pred[256,384]{1,0:T(8,128)(4,1)S(1)} %copy-done.6, f32[256,16]{0,1:T(8,128)S(1)} %bitcast.59), kind=kOutput, calls=%fused_computation.71 | convolution fusion | flops 107216896 | bytes 7471104 | tf_op jit(solution)/shard_map/hnc,chd->hnd/dot_general | solution.py:62
  48.1 1.9 %convolution_convert_fusion.4 = bf16[128,512]{1,0:T(8,128)(2,1)} fusion(bf16[128,512]{1,0:T(8,128)(2,1)S(1)} %copy-done.14, bf16[512,1536]{1,0:T(8,128)(2,1)} %param.20), kind=kOutput, calls=%fused_computation.56 | convolution fusion | flops 67174400 | bytes 786432 | tf_op jit(solution)/shard_map/dot_general | solution.py:37
  51.9 2.0 %maximum_select_fusion = bf16[512,1024]{1,0:T(8,128)(2,1)S(1)} fusion(bf16[256,1024]{1,0:T(8,128)(2,1)} %collective-permute-done.2, bf16[256,1024]{1,0:T(8,128)(2,1)} %slice.51, pred[]{:T(512)S(6)} %eq.35), kind=kLoop, calls=%fused_computation.67 | loop fusion | flops 4718592 | bytes 2097153 | tf_op jit(solution)/shard_map/jit(_where)/select_n | solution.py:118
  55.7 1.3 %copy.42 = bf16[512,512]{0,1:T(8,128)(2,1)S(1)} copy(bf16[512,512]{1,0:T(8,128)(2,1)} %get-tuple-element.4) | data formatting | bytes 1048576 | tf_op jit(solution)/shard_map/slice | solution.py:78
  57.0 1.4 %multiply_reduce_fusion = (f32[16,256]{1,0:T(8,128)S(1)}, f32[16,256,512]{2,1,0:T(8,128)S(1)}) fusion(bf16[256,16,32]{0,2,1:T(8,128)(2,1)S(1)} %bitcast.51, bf16[512,16,32]{0,2,1:T(8,128)(2,1)S(1)} %bitcast.48), kind=kOutput, calls=%fused_computation.5 | convolution fusion | flops 138407936 | bytes 9191424 | tf_op jit(solution)/shard_map/nhd,whd->hnw/dot_general | solution.py:82
  58.4 2.0 %fusion.2 = f32[16,256]{1,0:T(8,128)S(1)} fusion(f32[16,256,512]{2,1,0:T(8,128)S(1)} %get-tuple-element.13, f32[16,256]{1,0:T(8,128)S(1)} %get-tuple-element.12), kind=kLoop, calls=%fused_computation.6 | loop fusion | flops 6287360 | bytes 8421376 | tf_op jit(solution)/shard_map/reduce_sum | solution.py:83
  60.4 2.6 %fusion.30 = bf16[16,256,32]{1,2,0:T(8,128)(2,1)S(1)} fusion(bf16[512,16,32]{0,2,1:T(8,128)(2,1)S(1)} %bitcast.54, f32[16,256,512]{2,1,0:T(8,128)S(1)} %get-tuple-element.13, f32[16,256]{1,0:T(8,128)S(1)} %fusion.2, f32[16,256]{1,0:T(8,128)S(1)} %get-tuple-element.12), kind=kOutput, calls=%fused_computation.47 | convolution fusion | flops 140640256 | bytes 9207808 | tf_op jit(solution)/shard_map/hnw,whd->hnd/dot_general | solution.py:84
  63.4 2.0 %collective-permute-start.4 = (bf16[256,512]{1,0:T(8,128)(2,1)S(1)}, bf16[256,512]{1,0:T(8,128)(2,1)S(1)}, u32[]{:S(2)}, u32[]{:S(2)}) collective-permute-start(bf16[256,512]{1,0:T(8,128)(2,1)S(1)} %fusion.29), channel_id=1, source_target_pairs={{1,0},{2,1},{3,2},{4,3},{5,4},{6,5},{7,6},{8,7},{9,8},{10,9},{11,1... | collective-permute-start | bytes 786440 | tf_op jit(solution)/shard_map/ppermute | solution.py:20
  65.4 3.9 %collective-permute-start.3 = (bf16[256,512]{1,0:T(8,128)(2,1)S(1)}, bf16[256,512]{1,0:T(8,128)(2,1)S(1)}, u32[]{:S(2)}, u32[]{:S(2)}) collective-permute-start(bf16[256,512]{1,0:T(8,128)(2,1)S(1)} %fusion.29), channel_id=1, source_target_pairs={{0,1},{1,2},{2,3},{3,4},{4,5},{5,6},{6,7},{7,8},{8,9},{9,10},{10,1... | collective-permute-start | bytes 786440 | tf_op jit(solution)/shard_map/ppermute | solution.py:19
  71.1 1.2 %collective-permute-done.3 = bf16[256,512]{1,0:T(8,128)(2,1)S(1)} collective-permute-done((bf16[256,512]{1,0:T(8,128)(2,1)S(1)}, bf16[256,512]{1,0:T(8,128)(2,1)S(1)}, u32[]{:S(2)}, u32[]{:S(2)}) %collective-permute-start.3) | collective-permute-done | bytes 262176 | tf_op jit(solution)/shard_map/ppermute | solution.py:19
  72.9 2.3 %convolution_convert_fusion.1 = bf16[768,1024]{1,0:T(8,128)(2,1)S(1)} fusion(bf16[512,1536]{1,0:T(8,128)(2,1)} %param.20, f32[768]{0:T(1024)S(1)} %add_rsqrt_fusion, f32[768]{0:T(1024)S(1)} %broadcast_multiply_fusion, bf16[256,512]{1,0:T(8,128)(2,1)S(1)} %collective-permute-done.4, bf16[256,512]{1,0:T(8,128)(2,1)S(1)} %fusion.29, ...), kind=kOutput, calls=%fused_computation.35 | convolution fusion | flops 809631744 | bytes 3414016 | tf_op jit(solution)/shard_map/dot_general | solution.py:37
  76.2 2.3 %copy.45 = bf16[768,512]{0,1:T(8,128)(2,1)} copy(bf16[768,512]{1,0:T(8,128)(2,1)} %get-tuple-element.3) | data formatting | bytes 1572864 | tf_op jit(solution)/shard_map/slice | solution.py:53
  78.5 1.2 %copy.44 = bf16[768,512]{0,1:T(8,128)(2,1)} copy(bf16[768,512]{1,0:T(8,128)(2,1)S(1)} %get-tuple-element.2) | data formatting | bytes 1572864 | tf_op jit(solution)/shard_map/slice | solution.py:51
  79.7 2.5 %fusion.4 = (f32[16,128]{1,0:T(8,128)S(1)}, f32[16,128,768]{2,1,0:T(8,128)S(1)}) fusion(pred[128,768]{1,0:T(8,128)(4,1)} %broadcast_compare_fusion.1, bf16[128,16,32]{0,2,1:T(8,128)(2,1)} %bitcast.53, bf16[768,16,32]{0,2,1:T(8,128)(2,1)} %bitcast.47), kind=kOutput, calls=%fused_computation.12 | convolution fusion | flops 105379840 | bytes 7315456 | tf_op jit(solution)/shard_map/nhd,chd->hnc/dot_general | solution.py:55
  82.2 1.9 %fusion.7 = f32[16,128]{1,0:T(8,128)S(1)} fusion(f32[16,128,768]{2,1,0:T(8,128)S(1)} %get-tuple-element.15, f32[16,128]{1,0:T(8,128)S(1)} %get-tuple-element.14, f32[128,768]{1,0:T(8,128)S(1)} %convert_reduce_fusion.2, pred[128,768]{1,0:T(8,128)(4,1)S(1)} %copy-done.5), kind=kLoop, calls=%fused_computation.15 | loop fusion | flops 7862272 | bytes 6799360 | tf_op jit(solution)/shard_map/reduce_sum | solution.py:61
  84.2 2.1 %fusion.38 = bf16[128,16,32]{0,2,1:T(8,128)(2,1)S(1)} fusion(bf16[768,16,32]{0,2,1:T(8,128)(2,1)S(1)} %bitcast.52, f32[16,128,768]{2,1,0:T(8,128)S(1)} %get-tuple-element.15, f32[16,128]{1,0:T(8,128)S(1)} %get-tuple-element.14, f32[128,768]{1,0:T(8,128)S(1)} %convert_reduce_fusion.2, pred[128,768]{1,0:T(8,128)(4,1)S(1)} %copy-done.5, f32[128,16]{0,1:T(8,128)S(1)} %bitcast.60), kind=kOutput, calls=%fused_computation.58 | convolution fusion | flops 107085824 | bytes 7716864 | tf_op jit(solution)/shard_map/hnc,chd->hnd/dot_general | solution.py:62
  86.9 3.2 %fusion.36 = bf16[128,512]{1,0:T(8,128)(2,1)} fusion(f32[128,512]{1,0:T(8,128)S(1)} %get-tuple-element.17, bf16[2048,512]{1,0:T(8,128)(2,1)S(1)} %copy-done, bf16[512,2048]{1,0:T(8,128)(2,1)} %param.22, f32[128]{0:T(128)S(1)} %add_rsqrt_fusion.3, f32[128]{0:T(128)S(1)} %broadcast_multiply_fusion.3), kind=kOutput, calls=%fused_computation.55 | convolution fusion | flops 539557888 | bytes 4588544 | tf_op jit(solution)/shard_map/dot_general | solution.py:37
  (79 shorter events, 19.1 us)
Async XLA Ops:
  0.6 86.2 %copy-start = (bf16[2048,512]{1,0:T(8,128)(2,1)S(1)}, bf16[2048,512]{1,0:T(8,128)(2,1)}, u32[]{:S(2)}) copy-start(bf16[2048,512]{1,0:T(8,128)(2,1)} %param.23) | copy-start | bytes 6291460
  3.9 32.0 %copy-start.13 = (bf16[128,512]{1,0:T(8,128)(2,1)}, bf16[128,512]{1,0:T(8,128)(2,1)S(1)}, u32[]{:S(2)}) copy-start(bf16[128,512]{1,0:T(8,128)(2,1)S(1)} %fusion.73) | copy-start | bytes 393220
  4.0 31.9 %collective-permute-start.1 = (bf16[128,512]{1,0:T(8,128)(2,1)S(1)}, bf16[128,512]{1,0:T(8,128)(2,1)S(1)}, u32[]{:S(2)}, u32[]{:S(2)}) collective-permute-start(bf16[128,512]{1,0:T(8,128)(2,1)S(1)} %fusion.73), channel_id=1, source_target_pairs={{1,0},{2,1},{3,2},{4,3},{5,4},{6,5},{7,6},{8,7},{9,8},{10,9},{11,1... | collective-permute-start | bytes 393224 | tf_op jit(solution)/shard_map/ppermute | solution.py:20
  26.3 9.6 %collective-permute-start = (bf16[128,512]{1,0:T(8,128)(2,1)S(1)}, bf16[128,512]{1,0:T(8,128)(2,1)S(1)}, u32[]{:S(2)}, u32[]{:S(2)}) collective-permute-start(bf16[128,512]{1,0:T(8,128)(2,1)S(1)} %fusion.73), channel_id=1, source_target_pairs={{0,1},{1,2},{2,3},{3,4},{4,5},{5,6},{6,7},{7,8},{8,9},{9,10},{10,1... | collective-permute-start | bytes 393224 | tf_op jit(solution)/shard_map/ppermute | solution.py:19
  38.9 2.3 %copy-start.6 = (pred[256,384]{1,0:T(8,128)(4,1)S(1)}, pred[256,384]{1,0:T(8,128)(4,1)}, u32[]{:S(2)}) copy-start(pred[256,384]{1,0:T(8,128)(4,1)} %broadcast_compare_fusion) | copy-start | bytes 294916
  38.9 4.4 %copy-start.12 = (bf16[384,512]{0,1:T(8,128)(2,1)S(1)}, bf16[384,512]{0,1:T(8,128)(2,1)}, u32[]{:S(2)}) copy-start(bf16[384,512]{0,1:T(8,128)(2,1)} %copy.40) | copy-start | bytes 1179652
  43.3 2.1 %copy-start.2 = (bf16[256,512]{1,0:T(8,128)(2,1)S(1)}, bf16[256,512]{1,0:T(8,128)(2,1)}, u32[]{:S(2)}) copy-start(bf16[256,512]{1,0:T(8,128)(2,1)} %param.13) | copy-start | bytes 786436
  43.3 2.1 %copy-start.11 = (bf16[512,512]{1,0:T(8,128)(2,1)S(1)}, bf16[512,512]{1,0:T(8,128)(2,1)}, u32[]{:S(2)}) copy-start(bf16[512,512]{1,0:T(8,128)(2,1)} %param.17) | copy-start | bytes 1572868
  43.4 2.7 %copy-start.4 = (bf16[512,1536]{1,0:T(8,128)(2,1)S(1)}, bf16[512,1536]{1,0:T(8,128)(2,1)}, u32[]{:S(2)}) copy-start(bf16[512,1536]{1,0:T(8,128)(2,1)} %param.18) | copy-start | bytes 4718596
  43.4 4.7 %copy-start.16 = (s32[128,3]{0,1:T(4,128)S(1)}, s32[128,3]{0,1:T(4,128)}, u32[]{:S(2)}) copy-start(s32[128,3]{0,1:T(4,128)} %param.15) | copy-start | bytes 4612
  43.4 4.7 %copy-start.14 = (bf16[128,512]{1,0:T(8,128)(2,1)S(1)}, bf16[128,512]{1,0:T(8,128)(2,1)}, u32[]{:S(2)}) copy-start(bf16[128,512]{1,0:T(8,128)(2,1)} %copy-done.13) | copy-start | bytes 393220
  47.6 4.3 %collective-permute-start.2 = (bf16[256,1024]{1,0:T(8,128)(2,1)}, bf16[256,1024]{1,0:T(8,128)(2,1)}, u32[]{:S(2)}, u32[]{:S(2)}) collective-permute-start(bf16[256,1024]{1,0:T(8,128)(2,1)} %slice.51), channel_id=1, source_target_pairs={{0,1},{1,0},{2,3},{3,2},{4,5},{5,4},{6,7},{7,6},{8,9},{9,8},{10,11... | collective-permute-start | bytes 1572872 | tf_op jit(solution)/shard_map/ppermute | solution.py:26
  58.4 2.0 %copy-start.9 = (bf16[512,512]{0,1:T(8,128)(2,1)S(1)}, bf16[512,512]{0,1:T(8,128)(2,1)}, u32[]{:S(2)}) copy-start(bf16[512,512]{0,1:T(8,128)(2,1)} %copy.43) | copy-start | bytes 1572868
  60.4 2.7 %copy-start.8 = (bf16[512,512]{1,0:T(8,128)(2,1)S(1)}, bf16[512,512]{1,0:T(8,128)(2,1)}, u32[]{:S(2)}) copy-start(bf16[512,512]{1,0:T(8,128)(2,1)} %param.19) | copy-start | bytes 1572868
  60.4 9.0 %copy-start.15 = (bf16[128,512]{1,0:T(8,128)(2,1)S(1)}, bf16[128,512]{1,0:T(8,128)(2,1)}, u32[]{:S(2)}) copy-start(bf16[128,512]{1,0:T(8,128)(2,1)} %convolution_convert_fusion.4) | copy-start | bytes 393220
  63.4 15.1 %copy-start.1 = (bf16[256,512]{1,0:T(8,128)(2,1)}, bf16[256,512]{1,0:T(8,128)(2,1)S(1)}, u32[]{:S(2)}) copy-start(bf16[256,512]{1,0:T(8,128)(2,1)S(1)} %fusion.29) | copy-start | bytes 786436
  63.4 7.7 %collective-permute-start.4 = (bf16[256,512]{1,0:T(8,128)(2,1)S(1)}, bf16[256,512]{1,0:T(8,128)(2,1)S(1)}, u32[]{:S(2)}, u32[]{:S(2)}) collective-permute-start(bf16[256,512]{1,0:T(8,128)(2,1)S(1)} %fusion.29), channel_id=1, source_target_pairs={{1,0},{2,1},{3,2},{4,3},{5,4},{6,5},{7,6},{8,7},{9,8},{10,9},{11,1... | collective-permute-start | bytes 786440 | tf_op jit(solution)/shard_map/ppermute | solution.py:20
  65.4 7.0 %collective-permute-start.3 = (bf16[256,512]{1,0:T(8,128)(2,1)S(1)}, bf16[256,512]{1,0:T(8,128)(2,1)S(1)}, u32[]{:S(2)}, u32[]{:S(2)}) collective-permute-start(bf16[256,512]{1,0:T(8,128)(2,1)S(1)} %fusion.29), channel_id=1, source_target_pairs={{0,1},{1,2},{2,3},{3,4},{4,5},{5,6},{6,7},{7,8},{8,9},{9,10},{10,1... | collective-permute-start | bytes 786440 | tf_op jit(solution)/shard_map/ppermute | solution.py:19
  78.5 3.7 %copy-start.5 = (pred[128,768]{1,0:T(8,128)(4,1)S(1)}, pred[128,768]{1,0:T(8,128)(4,1)}, u32[]{:S(2)}) copy-start(pred[128,768]{1,0:T(8,128)(4,1)} %broadcast_compare_fusion.1) | copy-start | bytes 294916
  79.7 4.5 %copy-start.7 = (bf16[768,512]{0,1:T(8,128)(2,1)S(1)}, bf16[768,512]{0,1:T(8,128)(2,1)}, u32[]{:S(2)}) copy-start(bf16[768,512]{0,1:T(8,128)(2,1)} %copy.45) | copy-start | bytes 2359300
  84.2 2.1 %copy-start.3 = (bf16[128,512]{1,0:T(8,128)(2,1)S(1)}, bf16[128,512]{1,0:T(8,128)(2,1)}, u32[]{:S(2)}) copy-start(bf16[128,512]{1,0:T(8,128)(2,1)} %param.12) | copy-start | bytes 393220
  84.2 2.1 %copy-start.10 = (bf16[512,512]{1,0:T(8,128)(2,1)S(1)}, bf16[512,512]{1,0:T(8,128)(2,1)}, u32[]{:S(2)}) copy-start(bf16[512,512]{1,0:T(8,128)(2,1)} %param.21) | copy-start | bytes 1572868
where the time goes:
time: 90.8 us; the launch traced here: 90.1 us
  starting transfers between devices  30.6 us (34%)
  matrix products  25.3 us (28%)
  other arithmetic  18.9 us (21%)
  local copies, waits for them, and re-layouts  12.6 us (14%)
  waiting for transfers between devices  1.47 us (2%)
  between operations  1.15 us (1%)
    ppermute x2, starting transfers between devices, padded(): after = lax.ppermute(leading, axis, down)  24.3 us
    dot_general x9, matrix products, product(): return jnp.dot(left, right, preferred_element_type=jnp.float32)  12.3 us
    ppermute x2, starting transfers between devices, padded(): before = lax.ppermute(last, axis, up)  5.8 us
    dot_general x2, matrix products, dense_partial(): jnp.einsum('nhd,chd->hnc', query_heads, key_heads, preferred_element_type...  4.84 us
    dot_general x2, matrix products, dense_partial(): jnp.einsum('hnc,chd->hnd', weights, value_heads, preferred_element_type=j...  4.16 us
    reduce_sum x2, other arithmetic, dense_partial(): totals = jnp.sum(weights, axis=-1)  3.98 us
    slice x2, local copies, waits for them, and re-layouts, dense_partial(): key_values[:, model_width:].astype(jnp.float32)  3.19 us
    reduce_sum x5, other arithmetic, layer_norm(): spread = jnp.mean(center * center, axis=-1, keepdims=True)  3.02 us
  transfers between devices with their start and end apart: 5, of which 2 were waited for; matrix products, arithmetic and copies ran while one was open for 14% of the time, Pallas kernels for 0%

commit v1 on v0

v1 whole, which is shorter than its diff:
```python
import jax
import jax.numpy as jnp
from jax import lax
from jax.experimental import pallas as pl
from jax.experimental.pallas import tpu as pltpu
from jax.sharding import PartitionSpec as P

HEADS = 16
LANES = 128
EPSILON = 1e-05
LOG2E = 1.4426950408889634
MASKED = -1e30
BF16 = jnp.bfloat16
F32 = jnp.float32


def layer_norm(values):
    values = values.astype(F32)
    center = values - jnp.mean(values, axis=-1, keepdims=True)
    spread = jnp.mean(center * center, axis=-1, keepdims=True)
    return (center * lax.rsqrt(spread + EPSILON)).astype(BF16)


def dot(left, right):
    return jnp.dot(left, right, preferred_element_type=F32)


def dot_nt(left, right):
    return lax.dot_general(left, right, (((1,), (1,)), ((), ())), preferred_element_type=F32)


def lane_head(shape, head_size):
    return lax.broadcasted_iota(jnp.int32, shape, 1) // head_size


def block_columns(lists, pos, odd, rows):
    local = lists - pos * rows
    block = jnp.where(local < 0, -1, jnp.where(local < rows, 0, 1))
    inside = local - block * rows
    block = jnp.where(odd == 1, -block, block)
    return inside + jnp.where(block < 0, 2, block) * rows


def attend(q_ref, kv_ref, mix_ref, bias_ref=None):
    width = q_ref.shape[1]
    head_size = width // HEADS
    keys = kv_ref.shape[0]
    heads = lane_head((keys, LANES), head_size)
    zero = jnp.zeros((keys, LANES), BF16)
    one = jnp.ones((keys, LANES), BF16)
    for t in range(width // LANES):
        lanes = slice(t * LANES, (t + 1) * LANES)
        queries = q_ref[:, lanes]
        key_tile = kv_ref[:, lanes]
        value_tile = kv_ref[:, width + t * LANES : width + (t + 1) * LANES]
        total = None
        for h in range(LANES // head_size):
            chosen = heads == h
            scores = dot_nt(queries, jnp.where(chosen, key_tile, zero))
            if bias_ref is not None:
                scores = scores + bias_ref[...]
            weights = jnp.exp2(scores - jnp.max(scores, axis=1, keepdims=True)).astype(BF16)
            values = jnp.concatenate(
                [jnp.where(chosen, value_tile, zero), jnp.where(chosen, one, zero)], axis=1
            )
            part = dot(weights, values)
            total = part if total is None else total + part
        mix_ref[:, lanes] = (total[:, :LANES] / total[:, LANES:]).astype(BF16)


def prepare_kernel(
    pos_ref, grid_ref, hidden_ref, enc_nbr_ref, enc_qkv_ref, dec_qkv_ref,
    queries_ref, pairs_ref, bias_ref, dec_queries_ref,
):
    width = grid_ref.shape[1]
    rows = grid_ref.shape[0]
    scale = LOG2E / (width // HEADS) ** 0.5
    normed = layer_norm(grid_ref[...])
    pairs_ref[...] = dot(normed, enc_qkv_ref[:, width:]).astype(BF16)
    dec_queries_ref[...] = dot(normed, dec_qkv_ref[:, :width]).astype(BF16)
    queries = dot(layer_norm(hidden_ref[...]), enc_qkv_ref[:, :width])
    queries_ref[...] = (queries * scale).astype(BF16)
    pos = pos_ref[0]
    columns = block_columns(enc_nbr_ref[...], pos, pos % 2, rows)
    places = lax.broadcasted_iota(jnp.int32, bias_ref.shape, 1)
    counts = jnp.zeros(bias_ref.shape, F32)
    for k in range(columns.shape[1]):
        counts = counts + jnp.where(columns[:, k : k + 1] == places, 1.0, 0.0)
    bias_ref[...] = jnp.where(counts > 0.0, jnp.log2(jnp.maximum(counts, 1.0)), MASKED)


def encode_kernel(
    queries_ref, pairs_ref, bias_ref, partner_ref, off_ref, hidden_ref, qkv_ref, out_ref,
    result_ref, pairs, mix,
):
    width = hidden_ref.shape[1]
    rows = pairs_ref.shape[0]
    pairs[:rows] = pairs_ref[...]
    normed = jnp.concatenate([layer_norm(partner_ref[...]), layer_norm(off_ref[...])], axis=0)
    pairs[rows:] = dot(normed, qkv_ref[:, width:]).astype(BF16)
    attend(queries_ref, pairs, mix, bias_ref)
    result_ref[...] = (hidden_ref[...].astype(F32) + dot(mix[...], out_ref[...])).astype(BF16)


def project_kernel(hidden_ref, qkv_ref, queries_ref, pairs_ref):
    width = hidden_ref.shape[1]
    scale = LOG2E / (width // HEADS) ** 0.5
    normed = layer_norm(hidden_ref[...])
    queries_ref[...] = (dot(normed, qkv_ref[:, :width]) * scale).astype(BF16)
    pairs_ref[...] = dot(normed, qkv_ref[:, width:]).astype(BF16)


def process_kernel(queries_ref, pairs_ref, hidden_ref, partner_ref, qkv_ref, out_ref, result_ref, pairs, mix):
    width = hidden_ref.shape[1]
    rows = hidden_ref.shape[0]
    pairs[:rows] = pairs_ref[...]
    pairs[rows:] = dot(layer_norm(partner_ref[...]), qkv_ref[:, width:]).astype(BF16)
    attend(queries_ref, pairs, mix)
    result_ref[...] = (hidden_ref[...].astype(F32) + dot(mix[...], out_ref[...])).astype(BF16)


def decode_kernel(
    pos_ref, own_ref, partner_ref, off_ref, nbr_ref, queries_ref, grid_ref, qkv_ref, out_ref,
    mlp_in_ref, mlp_out_ref, result_ref, normed,
):
    width = own_ref.shape[1]
    head_size = width // HEADS
    rows = own_ref.shape[0]
    grid_rows = grid_ref.shape[0]
    slots = nbr_ref.shape[1]
    scale = LOG2E / head_size**0.5
    normed[:rows] = layer_norm(own_ref[...])
    normed[rows : 2 * rows] = layer_norm(partner_ref[...])
    normed[2 * rows :] = layer_norm(off_ref[...])
    pos = pos_ref[0]
    columns = block_columns(nbr_ref[...], pos, pos % 2, rows)
    places = lax.broadcasted_iota(jnp.int32, (grid_rows, 3 * rows), 1)
    picks = jnp.concatenate(
        [jnp.where(columns[:, j : j + 1] == places, 1.0, 0.0).astype(BF16) for j in range(slots)],
        axis=0,
    )
    rows_picked = dot(picks, normed[...]).astype(BF16)
    pairs = dot(rows_picked, qkv_ref[:, width:]).astype(BF16)
    feature = lax.broadcasted_iota(jnp.int32, (width, LANES), 0) // head_size
    heads = lax.broadcasted_iota(jnp.int32, (width, LANES), 1)
    gather_heads = jnp.where(feature == heads, 1.0, 0.0).astype(BF16)
    queries = queries_ref[...].astype(F32)
    scores = []
    for j in range(slots):
        keys = pairs[j * grid_rows : (j + 1) * grid_rows, :width].astype(F32)
        scores.append(dot((queries * keys).astype(BF16), gather_heads) * scale)
    maxima = scores[0]
    for j in range(1, slots):
        maxima = jnp.maximum(maxima, scores[j])
    weights = [jnp.exp2(s - maxima) for s in scores]
    total = weights[0]
    for j in range(1, slots):
        total = total + weights[j]
    mix = None
    for j in range(slots):
        spread = dot_nt((weights[j] / total).astype(BF16), gather_heads)
        part = spread * pairs[j * grid_rows : (j + 1) * grid_rows, width:].astype(F32)
        mix = part if mix is None else mix + part
    grid_one = (grid_ref[...].astype(F32) + dot(mix.astype(BF16), out_ref[...])).astype(BF16)
    inner = jax.nn.gelu(dot(layer_norm(grid_one), mlp_in_ref[...])).astype(BF16)
    result_ref[...] = (grid_one.astype(F32) + dot(inner, mlp_out_ref[...])).astype(BF16)


def call(kernel, outs, scratch, flops, *args, scalars=0):
    vmem = pl.BlockSpec(memory_space=pltpu.VMEM)
    smem = pl.BlockSpec(memory_space=pltpu.SMEM)
    return pl.pallas_call(
        kernel,
        out_shape=[jax.ShapeDtypeStruct(shape, kind) for shape, kind in outs],
        in_specs=[smem] * scalars + [vmem] * (len(args) - scalars),
        out_specs=[vmem] * len(outs),
        scratch_shapes=[pltpu.VMEM(shape, kind) for shape, kind in scratch],
        cost_estimate=pl.CostEstimate(flops=flops, transcendentals=0, bytes_accessed=0),
        compiler_params=pltpu.CompilerParams(vmem_limit_bytes=48 << 20),
        name=kernel.__name__,
    )(*args)


def local(
    grid, hidden, enc_nbr, dec_nbr, enc_qkv, enc_out, proc_qkv, proc_out, dec_qkv, dec_out,
    mlp_in, mlp_out,
):
    grid_rows, width = grid.shape
    rows = hidden.shape[0]
    devices = lax.axis_size("nodes")
    pos = lax.axis_index("nodes").astype(jnp.int32).reshape(1)
    inner_pairs = [(i, i ^ 1) for i in range(devices)]
    outer_pairs = [(i, i + 1) for i in range(1, devices - 1, 2)]
    outer_pairs = outer_pairs + [(j, i) for i, j in outer_pairs]

    def exchange(shard):
        off = lax.ppermute(shard, "nodes", outer_pairs)
        return lax.ppermute(shard, "nodes", inner_pairs), off

    grid_partner, grid_off = exchange(grid)
    queries, pairs, bias, dec_queries = call(
        prepare_kernel,
        [
            ((rows, width), BF16),
            ((grid_rows, 2 * width), BF16),
            ((rows, 3 * grid_rows), F32),
            ((grid_rows, width), BF16),
        ],
        [],
        2_000_000_000,
        pos, grid, hidden, enc_nbr, enc_qkv, dec_qkv,
        scalars=1,
    )
    (hidden_one,) = call(
        encode_kernel,
        [((rows, width), BF16)],
        [((3 * grid_rows, 2 * width), BF16), ((rows, width), BF16)],
        4_000_000_000,
        queries, pairs, bias, grid_partner, grid_off, hidden, enc_qkv, enc_out,
    )
    one_partner = lax.ppermute(hidden_one, "nodes", inner_pairs)
    queries, pairs = call(
        project_kernel,
        [((rows, width), BF16), ((rows, 2 * width), BF16)],
        [],
        1_000_000_000,
        hidden_one, proc_qkv,
    )
    (hidden_two,) = call(
        process_kernel,
        [((rows, width), BF16)],
        [((2 * rows, 2 * width), BF16), ((rows, width), BF16)],
        4_000_000_000,
        queries, pairs, hidden_one, one_partner, proc_qkv, proc_out,
    )
    two_partner, two_off = exchange(hidden_two)
    (grid_out,) = call(
        decode_kernel,
        [((grid_rows, width), BF16)],
        [((3 * rows, width), BF16)],
        4_000_000_000,
        pos, hidden_two, two_partner, two_off, dec_nbr, dec_queries, grid, dec_qkv, dec_out,
        mlp_in, mlp_out,
        scalars=1,
    )
    return (grid_out, hidden_two)


def solution(mesh):
    part = P(("groups", "nodes"), None)
    nodes = P("nodes", None)
    return jax.shard_map(
        local,
        mesh=mesh,
        in_specs=(part, part, nodes, nodes) + (P(),) * 8,
        out_specs=(part, part),
        check_vma=False,
    )
```

time: 90.8 us -> 56.3 us (0.62)
  matrix products: 25.3 us -> 0 us
  other arithmetic: 18.9 us -> 0 us
  Pallas kernels: 0 us -> 15.8 us
  local copies, waits for them, and re-layouts: 12.6 us -> 8.02 us
  starting transfers between devices: 30.6 us -> 26.4 us
  waiting for transfers between devices: 1.47 us -> 4.87 us
    dot_general x15 -> x0, matrix products: 25.3 us -> none  [the longest x9 12.3 us: product(): return jnp.dot(left, right, preferred_element_type=jnp.float32)]
    pallas_call x0 -> x5, Pallas kernels: none -> 15.8 us  [call(): pl.pallas_call(kernel, out_shape=[jax.ShapeDtypeStruct(shape, kind) for s...]
    reduce_sum x13 -> x0, other arithmetic: 13.8 us -> none  [the longest x2 3.98 us: dense_partial(): totals = jnp.sum(weights, axis=-1)]
    slice x12 -> x0, local copies, waits for them, and re-layouts: 11.5 us -> none  [the longest x2 3.19 us: dense_partial(): key_values[:, model_width:].astype(jnp.float32)]
    unnamed x34 -> x30, local copies, waits for them, and re-layouts: 0.11 us -> 8.02 us
    ppermute x5, starting transfers between devices: 30.6 us -> 26.4 us  [the longest x2 20.7 us: exchange(): return (lax.ppermute(shard, 'nodes', inner_pairs), off)]
    ppermute x5, waiting for transfers between devices: 1.47 us -> 4.87 us  [the longest x2 4.13 us: exchange(): off = lax.ppermute(shard, 'nodes', outer_pairs)]
    select_n x1 -> x0, other arithmetic: 1.97 us -> none  [local(): jnp.where(lower_half, jnp.concatenate([window_pairs, partner], axis=0), j...]
  transfers between devices with their start and end apart: 5 -> 5, of which waited for: 2 -> 2; matrix products, arithmetic and copies ran while one was open for 14% -> 2% of each run, Pallas kernels for 0% -> 5%
where the time goes in v1:
time: 56.3 us; the launch traced here: 55.9 us
  starting transfers between devices  26.4 us (47%)
  Pallas kernels  15.8 us (28%)
  local copies, waits for them, and re-layouts  8.02 us (14%)
  waiting for transfers between devices  4.87 us (9%)
  between operations  0.79 us (1%)
    ppermute x2, starting transfers between devices, exchange(): return (lax.ppermute(shard, 'nodes', inner_pairs), off)  20.7 us
    pallas_call x5, Pallas kernels, call(): pl.pallas_call(kernel, out_shape=[jax.ShapeDtypeStruct(shape, kind) for s...  15.8 us
    unnamed x30, local copies, waits for them, and re-layouts  8.02 us
    ppermute x2, starting transfers between devices, exchange(): off = lax.ppermute(shard, 'nodes', outer_pairs)  5.6 us
    ppermute x2, waiting for transfers between devices, exchange(): off = lax.ppermute(shard, 'nodes', outer_pairs)  4.13 us
  transfers between devices with their start and end apart: 5, of which 2 were waited for; matrix products, arithmetic and copies ran while one was open for 2% of the time, Pallas kernels for 5%

profile of v1, /device:TPU:33, one launch (start us, length us, event | category | flops | bytes accessed | tf_op | source)
XLA Modules:
  0.0 55.9 jit_solution(12789847742988467010)
XLA Ops:
  0.6 20.5 %collective-permute-start = (bf16[128,512]{1,0:T(8,128)(2,1)}, bf16[128,512]{1,0:T(8,128)(2,1)S(1)}, u32[]{:S(2)}, u32[]{:S(2)}) collective-permute-start(bf16[128,512]{1,0:T(8,128)(2,1)} %grid_ref.3), channel_id=1, source_target_pairs={{0,1},{1,0},{2,3},{3,2},{4,5},{5,4},{6,7},{7,6},{8,9},{9,8},{10,11... | collective-permute-start | bytes 393224 | tf_op jit(solution)/shard_map/ppermute | solution.py:198
  21.2 1.9 %collective-permute-start.1 = (bf16[128,512]{1,0:T(8,128)(2,1)}, bf16[128,512]{1,0:T(8,128)(2,1)S(1)}, u32[]{:S(2)}, u32[]{:S(2)}) collective-permute-start(bf16[128,512]{1,0:T(8,128)(2,1)} %grid_ref.3), channel_id=1, source_target_pairs={{1,2},{3,4},{5,6},{7,8},{9,10},{11,12},{13,14},{15,16},{17,18},{19... | collective-permute-start | bytes 393224 | tf_op jit(solution)/shard_map/ppermute | solution.py:197
  23.1 0.9 %copy.14.enc_nbr_ref = s32[256,32]{1,0:T(8,128)S(1)} copy(s32[256,32]{0,1:T(8,128)} %param.14) | data formatting | bytes 65536 | tf_op args[2]
  24.0 1.4 %copy-done.1 = bf16[512,1536]{1,0:T(8,128)(2,1)S(1)} copy-done((bf16[512,1536]{1,0:T(8,128)(2,1)S(1)}, bf16[512,1536]{1,0:T(8,128)(2,1)}, u32[]{:S(2)}) %copy-start.1) | copy-done | bytes 1572888
  25.4 1.4 %copy-done.4 = bf16[512,1536]{1,0:T(8,128)(2,1)S(1)} copy-done((bf16[512,1536]{1,0:T(8,128)(2,1)S(1)}, bf16[512,1536]{1,0:T(8,128)(2,1)}, u32[]{:S(2)}) %copy-start.4) | copy-done | bytes 1572888
  26.8 0.9 %copy-done.9 = bf16[256,512]{1,0:T(8,128)(2,1)S(1)} copy-done((bf16[256,512]{1,0:T(8,128)(2,1)S(1)}, bf16[256,512]{1,0:T(8,128)(2,1)}, u32[]{:S(2)}) %copy-start.9) | copy-done | bytes 262168
  27.7 0.9 %copy-done.11 = bf16[128,512]{1,0:T(8,128)(2,1)S(1)} copy-done((bf16[128,512]{1,0:T(8,128)(2,1)S(1)}, bf16[128,512]{1,0:T(8,128)(2,1)}, u32[]{:S(2)}) %copy-start.11) | copy-done | bytes 131096
  28.7 2.0 %prepare_kernel.1 = (bf16[256,512]{1,0:T(8,128)(2,1)S(1)}, bf16[128,1024]{1,0:T(8,128)(2,1)S(1)}, f32[256,384]{1,0:T(8,128)S(1)}, bf16[128,512]{1,0:T(8,128)(2,1)S(1)}) custom-call(s32[1]{0:T(128)} %bitcast.pos_ref, bf16[128,512]{1,0:T(8,128)(2,1)S(1)} %copy-done.11, bf16[256,512]{1,0:T(8,128)(2,1)S(1)} %copy-done.9, s32[256,32]{1,0:T(8,128)S(1)} %copy.14.enc_nbr_ref, ...), custom_call_target="tpu_custom_call" | custom-call | flops 2000000000 | tf_op jit(solution)/shard_map/prepare_kernel/pallas_call | solution.py:172
  30.7 0.0 copy-start.3
  30.7 3.6 %encode_kernel.1.hidden_ref = bf16[256,512]{1,0:T(8,128)(2,1)S(1)} custom-call(bf16[256,512]{1,0:T(8,128)(2,1)S(1)} %get-tuple-element.8.queries_ref, bf16[128,1024]{1,0:T(8,128)(2,1)S(1)} %get-tuple-element.9.pairs_ref, f32[256,384]{1,0:T(8,128)S(1)} %get-tuple-element.10.bias_ref, bf16[128,512]{1,0:T(8,128)(2,1)S(1)} %collective-permute-done.partner_ref, ...), custom_call_target="tpu_custom_call" | custom-call | flops 4000000000 | tf_op jit(solution)/shard_map/encode_kernel/pallas_call | solution.py:172
  34.2 0.0 copy-start.7
  34.3 0.1 collective-permute-start.2
  34.4 0.8 %project_kernel.1 = (bf16[256,512]{1,0:T(8,128)(2,1)S(1)}, bf16[256,1024]{1,0:T(8,128)(2,1)S(1)}) custom-call(bf16[256,512]{1,0:T(8,128)(2,1)S(1)} %encode_kernel.1.hidden_ref, bf16[512,1536]{1,0:T(8,128)(2,1)S(1)} %copy-done.3), custom_call_target="tpu_custom_call" | custom-call | flops 1000000000 | tf_op jit(solution)/shard_map/project_kernel/pallas_call | solution.py:172
  35.2 0.7 %collective-permute-done.2.partner_ref = bf16[256,512]{1,0:T(8,128)(2,1)S(1)} collective-permute-done((bf16[256,512]{1,0:T(8,128)(2,1)S(1)}, bf16[256,512]{1,0:T(8,128)(2,1)S(1)}, u32[]{:S(2)}, u32[]{:S(2)}) %collective-permute-start.2) | collective-permute-done | bytes 262176 | tf_op jit(solution)/shard_map/ppermute | solution.py:221
  35.9 0.0 copy-start.12
  35.9 4.3 %process_kernel.1.own_ref = bf16[256,512]{1,0:T(8,128)(2,1)} custom-call(bf16[256,512]{1,0:T(8,128)(2,1)S(1)} %get-tuple-element.11.queries_ref, bf16[256,1024]{1,0:T(8,128)(2,1)S(1)} %get-tuple-element.12.pairs_ref, bf16[256,512]{1,0:T(8,128)(2,1)S(1)} %encode_kernel.1.hidden_ref, bf16[256,512]{1,0:T(8,128)(2,1)S(1)} %collective-permute-done.2.partner_ref, ...), custom_call_target="tpu_custom_call" | custom-call | flops 4000000000 | tf_op jit(solution)/shard_map/process_kernel/pallas_call | solution.py:172
  40.3 0.1 collective-permute-start.3
  40.4 3.7 %collective-permute-start.4 = (bf16[256,512]{1,0:T(8,128)(2,1)}, bf16[256,512]{1,0:T(8,128)(2,1)S(1)}, u32[]{:S(2)}, u32[]{:S(2)}) collective-permute-start(bf16[256,512]{1,0:T(8,128)(2,1)} %process_kernel.1.own_ref), channel_id=1, source_target_pairs={{1,2},{3,4},{5,6},{7,8},{9,10},{11,12},{13,14},{15,16},{17,18},{19... | collective-permute-start | bytes 786440 | tf_op jit(solution)/shard_map/ppermute | solution.py:197
  44.1 0.1 copy.15.nbr_ref
  44.2 4.1 %collective-permute-done.4.off_ref = bf16[256,512]{1,0:T(8,128)(2,1)S(1)} collective-permute-done((bf16[256,512]{1,0:T(8,128)(2,1)}, bf16[256,512]{1,0:T(8,128)(2,1)S(1)}, u32[]{:S(2)}, u32[]{:S(2)}) %collective-permute-start.4) | collective-permute-done | bytes 262176 | tf_op jit(solution)/shard_map/ppermute | solution.py:197
  48.3 0.0 copy-start.5
  48.3 1.4 %copy-done.5 = bf16[512,1536]{1,0:T(8,128)(2,1)S(1)} copy-done((bf16[512,1536]{1,0:T(8,128)(2,1)S(1)}, bf16[512,1536]{1,0:T(8,128)(2,1)}, u32[]{:S(2)}) %copy-start.5) | copy-done | bytes 1572888
  49.7 0.9 %copy-done.10 = bf16[256,512]{1,0:T(8,128)(2,1)S(1)} copy-done((bf16[256,512]{1,0:T(8,128)(2,1)S(1)}, bf16[256,512]{1,0:T(8,128)(2,1)}, u32[]{:S(2)}) %copy-start.10) | copy-done | bytes 262168
  50.7 5.2 %decode_kernel.1 = bf16[128,512]{1,0:T(8,128)(2,1)} custom-call(s32[1]{0:T(128)} %bitcast.pos_ref, bf16[256,512]{1,0:T(8,128)(2,1)S(1)} %copy-done.10, bf16[256,512]{1,0:T(8,128)(2,1)S(1)} %collective-permute-done.3.partner_ref, bf16[256,512]{1,0:T(8,128)(2,1)S(1)} %collective-permute-done.4.off_ref, s32[128,3]{1,0:T(8,128)S(1)} %copy.15.nbr_ref, ...), custom_call_target="tpu_custom_call" | custom-call | flops 4000000000 | tf_op jit(solution)/shard_map/decode_kernel/pallas_call | solution.py:172
  (21 shorter events, 0.0 us)
Async XLA Ops:
  0.6 30.0 %collective-permute-start = (bf16[128,512]{1,0:T(8,128)(2,1)}, bf16[128,512]{1,0:T(8,128)(2,1)S(1)}, u32[]{:S(2)}, u32[]{:S(2)}) collective-permute-start(bf16[128,512]{1,0:T(8,128)(2,1)} %grid_ref.3), channel_id=1, source_target_pairs={{0,1},{1,0},{2,3},{3,2},{4,5},{5,4},{6,7},{7,6},{8,9},{9,8},{10,11... | collective-permute-start | bytes 393224 | tf_op jit(solution)/shard_map/ppermute | solution.py:198
  21.2 9.5 %collective-permute-start.1 = (bf16[128,512]{1,0:T(8,128)(2,1)}, bf16[128,512]{1,0:T(8,128)(2,1)S(1)}, u32[]{:S(2)}, u32[]{:S(2)}) collective-permute-start(bf16[128,512]{1,0:T(8,128)(2,1)} %grid_ref.3), channel_id=1, source_target_pairs={{1,2},{3,4},{5,6},{7,8},{9,10},{11,12},{13,14},{15,16},{17,18},{19... | collective-permute-start | bytes 393224 | tf_op jit(solution)/shard_map/ppermute | solution.py:197
  24.0 1.4 %copy-start.1 = (bf16[512,1536]{1,0:T(8,128)(2,1)S(1)}, bf16[512,1536]{1,0:T(8,128)(2,1)}, u32[]{:S(2)}) copy-start(bf16[512,1536]{1,0:T(8,128)(2,1)} %qkv_ref.4) | copy-start | bytes 4718596
  25.4 1.4 %copy-start.4 = (bf16[512,1536]{1,0:T(8,128)(2,1)S(1)}, bf16[512,1536]{1,0:T(8,128)(2,1)}, u32[]{:S(2)}) copy-start(bf16[512,1536]{1,0:T(8,128)(2,1)} %qkv_ref.7) | copy-start | bytes 4718596
  26.8 0.9 %copy-start.9 = (bf16[256,512]{1,0:T(8,128)(2,1)S(1)}, bf16[256,512]{1,0:T(8,128)(2,1)}, u32[]{:S(2)}) copy-start(bf16[256,512]{1,0:T(8,128)(2,1)} %hidden_ref.3) | copy-start | bytes 786436
  27.7 0.9 %copy-start.11 = (bf16[128,512]{1,0:T(8,128)(2,1)S(1)}, bf16[128,512]{1,0:T(8,128)(2,1)}, u32[]{:S(2)}) copy-start(bf16[128,512]{1,0:T(8,128)(2,1)} %grid_ref.3) | copy-start | bytes 393220
  28.6 2.0 %copy-start.2 = (bf16[512,1536]{1,0:T(8,128)(2,1)S(1)}, bf16[512,1536]{1,0:T(8,128)(2,1)}, u32[]{:S(2)}) copy-start(bf16[512,1536]{1,0:T(8,128)(2,1)} %qkv_ref.4) | copy-start | bytes 4718596
  28.7 2.0 %copy-start.6 = (bf16[512,512]{1,0:T(8,128)(2,1)S(1)}, bf16[512,512]{1,0:T(8,128)(2,1)}, u32[]{:S(2)}) copy-start(bf16[512,512]{1,0:T(8,128)(2,1)} %out_ref.3) | copy-start | bytes 1572868
  30.7 3.7 %copy-start.3 = (bf16[512,1536]{1,0:T(8,128)(2,1)S(1)}, bf16[512,1536]{1,0:T(8,128)(2,1)}, u32[]{:S(2)}) copy-start(bf16[512,1536]{1,0:T(8,128)(2,1)} %qkv_ref.6) | copy-start | bytes 4718596
  34.2 1.7 %copy-start.7 = (bf16[512,512]{1,0:T(8,128)(2,1)S(1)}, bf16[512,512]{1,0:T(8,128)(2,1)}, u32[]{:S(2)}) copy-start(bf16[512,512]{1,0:T(8,128)(2,1)} %out_ref.4) | copy-start | bytes 1572868
  34.3 1.7 %collective-permute-start.2 = (bf16[256,512]{1,0:T(8,128)(2,1)S(1)}, bf16[256,512]{1,0:T(8,128)(2,1)S(1)}, u32[]{:S(2)}, u32[]{:S(2)}) collective-permute-start(bf16[256,512]{1,0:T(8,128)(2,1)S(1)} %encode_kernel.1.hidden_ref), channel_id=1, source_target_pairs={{0,1},{1,0},{2,3},{3,2},{4,5},{5,4},{6,7},{7,6},{8,9},{9,8},{10,11... | collective-permute-start | bytes 786440 | tf_op jit(solution)/shard_map/ppermute | solution.py:221
  35.9 8.2 %copy-start.13 = (s32[128,3]{0,1:T(4,128)S(1)}, s32[128,3]{0,1:T(4,128)}, u32[]{:S(2)}) copy-start(s32[128,3]{0,1:T(4,128)} %param.15) | copy-start | bytes 4612
  35.9 12.4 %copy-start = (bf16[512,2048]{1,0:T(8,128)(2,1)S(1)}, bf16[512,2048]{1,0:T(8,128)(2,1)}, u32[]{:S(2)}) copy-start(bf16[512,2048]{1,0:T(8,128)(2,1)} %mlp_in_ref.1) | copy-start | bytes 6291460
  35.9 12.4 %copy-start.8 = (bf16[512,512]{1,0:T(8,128)(2,1)S(1)}, bf16[512,512]{1,0:T(8,128)(2,1)}, u32[]{:S(2)}) copy-start(bf16[512,512]{1,0:T(8,128)(2,1)} %out_ref.5) | copy-start | bytes 1572868
  35.9 12.4 %copy-start.12 = (bf16[128,512]{1,0:T(8,128)(2,1)S(1)}, bf16[128,512]{1,0:T(8,128)(2,1)}, u32[]{:S(2)}) copy-start(bf16[128,512]{1,0:T(8,128)(2,1)} %grid_ref.3) | copy-start | bytes 393220
  40.3 3.9 %collective-permute-start.3 = (bf16[256,512]{1,0:T(8,128)(2,1)}, bf16[256,512]{1,0:T(8,128)(2,1)S(1)}, u32[]{:S(2)}, u32[]{:S(2)}) collective-permute-start(bf16[256,512]{1,0:T(8,128)(2,1)} %process_kernel.1.own_ref), channel_id=1, source_target_pairs={{0,1},{1,0},{2,3},{3,2},{4,5},{5,4},{6,7},{7,6},{8,9},{9,8},{10,11... | collective-permute-start | bytes 786440 | tf_op jit(solution)/shard_map/ppermute | solution.py:198
  40.4 7.9 %collective-permute-start.4 = (bf16[256,512]{1,0:T(8,128)(2,1)}, bf16[256,512]{1,0:T(8,128)(2,1)S(1)}, u32[]{:S(2)}, u32[]{:S(2)}) collective-permute-start(bf16[256,512]{1,0:T(8,128)(2,1)} %process_kernel.1.own_ref), channel_id=1, source_target_pairs={{1,2},{3,4},{5,6},{7,8},{9,10},{11,12},{13,14},{15,16},{17,18},{19... | collective-permute-start | bytes 786440 | tf_op jit(solution)/shard_map/ppermute | solution.py:197
  48.3 1.4 %copy-start.5 = (bf16[512,1536]{1,0:T(8,128)(2,1)S(1)}, bf16[512,1536]{1,0:T(8,128)(2,1)}, u32[]{:S(2)}) copy-start(bf16[512,1536]{1,0:T(8,128)(2,1)} %qkv_ref.7) | copy-start | bytes 4718596
  49.7 0.9 %copy-start.10 = (bf16[256,512]{1,0:T(8,128)(2,1)S(1)}, bf16[256,512]{1,0:T(8,128)(2,1)}, u32[]{:S(2)}) copy-start(bf16[256,512]{1,0:T(8,128)(2,1)} %process_kernel.1.own_ref) | copy-start | bytes 786436

commit v2 on v1

--- a/solution.py
+++ b/solution.py
@@ -69,24 +69,49 @@
 
 
 def prepare_kernel(
-    pos_ref, grid_ref, hidden_ref, enc_nbr_ref, enc_qkv_ref, dec_qkv_ref,
-    queries_ref, pairs_ref, bias_ref, dec_queries_ref,
+    pos_ref, grid_hbm, hidden_hbm, enc_nbr_hbm, enc_qkv_hbm,
+    queries_ref, pairs_ref, bias_ref,
+    grid_ref, hidden_ref, enc_nbr_ref, enc_qkv_ref, arrived,
 ):
     width = grid_ref.shape[1]
     rows = grid_ref.shape[0]
     scale = LOG2E / (width // HEADS) ** 0.5
-    normed = layer_norm(grid_ref[...])
-    pairs_ref[...] = dot(normed, enc_qkv_ref[:, width:]).astype(BF16)
-    dec_queries_ref[...] = dot(normed, dec_qkv_ref[:, :width]).astype(BF16)
-    queries = dot(layer_norm(hidden_ref[...]), enc_qkv_ref[:, :width])
-    queries_ref[...] = (queries * scale).astype(BF16)
+    copies = [
+        pltpu.make_async_copy(source, target, arrived.at[i])
+        for i, (source, target) in enumerate(
+            [
+                (enc_nbr_hbm, enc_nbr_ref),
+                (grid_hbm, grid_ref),
+                (hidden_hbm, hidden_ref),
+                (enc_qkv_hbm, enc_qkv_ref),
+            ]
+        )
+    ]
+    for copy in copies:
+        copy.start()
+    copies[0].wait()
     pos = pos_ref[0]
     columns = block_columns(enc_nbr_ref[...], pos, pos % 2, rows)
-    places = lax.broadcasted_iota(jnp.int32, bias_ref.shape, 1)
-    counts = jnp.zeros(bias_ref.shape, F32)
-    for k in range(columns.shape[1]):
-        counts = counts + jnp.where(columns[:, k : k + 1] == places, 1.0, 0.0)
-    bias_ref[...] = jnp.where(counts > 0.0, jnp.log2(jnp.maximum(counts, 1.0)), MASKED)
+    half = bias_ref.shape[1] // 2
+    columns = (columns - half).astype(F32).astype(BF16)
+    one = jnp.ones((rows, columns.shape[1]), BF16)
+    for b in range(bias_ref.shape[1] // rows):
+        places = b * rows - half + lax.broadcasted_iota(jnp.int32, one.shape, 0)
+        places = places.astype(F32).astype(BF16)
+        counts = jnp.zeros_like(one)
+        for k in range(columns.shape[0]):
+            counts = counts + jnp.where(columns[k : k + 1] == places, one, jnp.zeros_like(one))
+        counts = counts.astype(F32)
+        bias = jnp.where(counts > 0.0, jnp.log2(jnp.maximum(counts, 1.0)), MASKED)
+        bias_ref[:, b * rows : (b + 1) * rows] = bias.T
+    copies[1].wait()
+    copies[2].wait()
+    normed = layer_norm(grid_ref[...])
+    normed_hidden = layer_norm(hidden_ref[...])
+    copies[3].wait()
+    pairs_ref[...] = dot(normed, enc_qkv_ref[:, width:]).astype(BF16)
+    queries = dot(normed_hidden, enc_qkv_ref[:, :width])
+    queries_ref[...] = (queries * scale).astype(BF16)
 
 
 def encode_kernel(
@@ -119,27 +144,52 @@
     result_ref[...] = (hidden_ref[...].astype(F32) + dot(mix[...], out_ref[...])).astype(BF16)
 
 
-def decode_kernel(
-    pos_ref, own_ref, partner_ref, off_ref, nbr_ref, queries_ref, grid_ref, qkv_ref, out_ref,
-    mlp_in_ref, mlp_out_ref, result_ref, normed,
+def picks_of(columns, first, rows):
+    places = first + lax.broadcasted_iota(jnp.int32, (columns.shape[0], rows), 1)
+    return jnp.concatenate(
+        [
+            jnp.where(columns[:, j : j + 1] == places, 1.0, 0.0).astype(BF16)
+            for j in range(columns.shape[1])
+        ],
+        axis=0,
+    )
+
+
+def gather_kernel(
+    pos_ref, own_ref, partner_ref, nbr_ref, grid_hbm, qkv_hbm,
+    two_hbm, queries_ref, picked_ref, off_picks_ref, grid_ref,
+    normed, qkv_ref, arrived, written,
 ):
     width = own_ref.shape[1]
-    head_size = width // HEADS
     rows = own_ref.shape[0]
-    grid_rows = grid_ref.shape[0]
-    slots = nbr_ref.shape[1]
-    scale = LOG2E / head_size**0.5
-    normed[:rows] = layer_norm(own_ref[...])
-    normed[rows : 2 * rows] = layer_norm(partner_ref[...])
-    normed[2 * rows :] = layer_norm(off_ref[...])
+    grid_copy = pltpu.make_async_copy(grid_hbm, grid_ref, arrived.at[0])
+    qkv_copy = pltpu.make_async_copy(qkv_hbm.at[:, :width], qkv_ref, arrived.at[1])
+    copy = pltpu.make_async_copy(own_ref, two_hbm, written)
+    grid_copy.start()
+    qkv_copy.start()
+    copy.start()
     pos = pos_ref[0]
     columns = block_columns(nbr_ref[...], pos, pos % 2, rows)
-    places = lax.broadcasted_iota(jnp.int32, (grid_rows, 3 * rows), 1)
-    picks = jnp.concatenate(
-        [jnp.where(columns[:, j : j + 1] == places, 1.0, 0.0).astype(BF16) for j in range(slots)],
-        axis=0,
-    )
-    rows_picked = dot(picks, normed[...]).astype(BF16)
+    off_picks_ref[...] = picks_of(columns, 2 * rows, rows)
+    normed[:rows] = layer_norm(own_ref[...])
+    normed[rows:] = layer_norm(partner_ref[...])
+    picked_ref[...] = dot(picks_of(columns, 0, 2 * rows), normed[...]).astype(BF16)
+    grid_copy.wait()
+    qkv_copy.wait()
+    queries_ref[...] = dot(layer_norm(grid_ref[...]), qkv_ref[...]).astype(BF16)
+    copy.wait()
+
+
+def decode_kernel(
+    off_ref, off_picks_ref, picked_ref, queries_ref, grid_ref, qkv_ref, out_ref,
+    mlp_in_ref, mlp_out_ref, result_ref,
+):
+    width = off_ref.shape[1]
+    head_size = width // HEADS
+    grid_rows = grid_ref.shape[0]
+    slots = picked_ref.shape[0] // grid_rows
+    scale = LOG2E / head_size**0.5
+    rows_picked = picked_ref[...] + dot(off_picks_ref[...], layer_norm(off_ref[...])).astype(BF16)
     pairs = dot(rows_picked, qkv_ref[:, width:]).astype(BF16)
     feature = lax.broadcasted_iota(jnp.int32, (width, LANES), 0) // head_size
     heads = lax.broadcasted_iota(jnp.int32, (width, LANES), 1)
@@ -166,27 +216,34 @@
     result_ref[...] = (grid_one.astype(F32) + dot(inner, mlp_out_ref[...])).astype(BF16)
 
 
-def call(kernel, outs, scratch, flops, *args, scalars=0):
+def call(kernel, outs, scratch, flops, limit, *args, scalars=0, anywhere=(), out_anywhere=()):
     vmem = pl.BlockSpec(memory_space=pltpu.VMEM)
     smem = pl.BlockSpec(memory_space=pltpu.SMEM)
+    hbm = pl.BlockSpec(memory_space=pltpu.HBM)
+    args = [
+        pltpu.with_memory_space_constraint(x, pltpu.HBM) if i in anywhere else x
+        for i, x in enumerate(args)
+    ]
     return pl.pallas_call(
         kernel,
         out_shape=[jax.ShapeDtypeStruct(shape, kind) for shape, kind in outs],
-        in_specs=[smem] * scalars + [vmem] * (len(args) - scalars),
-        out_specs=[vmem] * len(outs),
-        scratch_shapes=[pltpu.VMEM(shape, kind) for shape, kind in scratch],
+        in_specs=[
+            smem if i < scalars else hbm if i in anywhere else vmem for i in range(len(args))
+        ],
+        out_specs=[hbm if i in out_anywhere else vmem for i in range(len(outs))],
+        scratch_shapes=scratch,
         cost_estimate=pl.CostEstimate(flops=flops, transcendentals=0, bytes_accessed=0),
-        compiler_params=pltpu.CompilerParams(vmem_limit_bytes=48 << 20),
-        name=kernel.__name__,
+        compiler_params=pltpu.CompilerParams(vmem_limit_bytes=limit << 20),
     )(*args)
 
 
-def local(
+def step(
     grid, hidden, enc_nbr, dec_nbr, enc_qkv, enc_out, proc_qkv, proc_out, dec_qkv, dec_out,
     mlp_in, mlp_out,
 ):
     grid_rows, width = grid.shape
     rows = hidden.shape[0]
+    slots = dec_nbr.shape[1]
     devices = lax.axis_size("nodes")
     pos = lax.axis_index("nodes").astype(jnp.int32).reshape(1)
     inner_pairs = [(i, i ^ 1) for i in range(devices)]
@@ -198,24 +255,28 @@
         return lax.ppermute(shard, "nodes", inner_pairs), off
 
     grid_partner, grid_off = exchange(grid)
-    queries, pairs, bias, dec_queries = call(
+    queries, pairs, bias = call(
         prepare_kernel,
+        [((rows, width), BF16), ((grid_rows, 2 * width), BF16), ((rows, 3 * grid_rows), F32)],
         [
-            ((rows, width), BF16),
-            ((grid_rows, 2 * width), BF16),
-            ((rows, 3 * grid_rows), F32),
-            ((grid_rows, width), BF16),
-        ],
-        [],
+            pltpu.VMEM(grid.shape, BF16),
+            pltpu.VMEM(hidden.shape, BF16),
+            pltpu.VMEM(enc_nbr.shape[::-1], jnp.int32),
+            pltpu.VMEM(enc_qkv.shape, BF16),
+            pltpu.SemaphoreType.DMA((4,)),
+        ],
         2_000_000_000,
-        pos, grid, hidden, enc_nbr, enc_qkv, dec_qkv,
+        16,
+        pos, grid, hidden, enc_nbr.T, enc_qkv,
         scalars=1,
+        anywhere=(1, 2, 3, 4),
     )
     (hidden_one,) = call(
         encode_kernel,
         [((rows, width), BF16)],
-        [((3 * grid_rows, 2 * width), BF16), ((rows, width), BF16)],
+        [pltpu.VMEM((3 * grid_rows, 2 * width), BF16), pltpu.VMEM((rows, width), BF16)],
         4_000_000_000,
+        16,
         queries, pairs, bias, grid_partner, grid_off, hidden, enc_qkv, enc_out,
     )
     one_partner = lax.ppermute(hidden_one, "nodes", inner_pairs)
@@ -224,24 +285,47 @@
         [((rows, width), BF16), ((rows, 2 * width), BF16)],
         [],
         1_000_000_000,
+        16,
         hidden_one, proc_qkv,
     )
-    (hidden_two,) = call(
+    (two_near,) = call(
         process_kernel,
         [((rows, width), BF16)],
-        [((2 * rows, 2 * width), BF16), ((rows, width), BF16)],
+        [pltpu.VMEM((2 * rows, 2 * width), BF16), pltpu.VMEM((rows, width), BF16)],
         4_000_000_000,
+        16,
         queries, pairs, hidden_one, one_partner, proc_qkv, proc_out,
     )
-    two_partner, two_off = exchange(hidden_two)
+    two_partner, two_off = exchange(two_near)
+    hidden_two, dec_queries, picked, off_picks, grid_near = call(
+        gather_kernel,
+        [
+            ((rows, width), BF16),
+            ((grid_rows, width), BF16),
+            ((slots * grid_rows, width), BF16),
+            ((slots * grid_rows, rows), BF16),
+            ((grid_rows, width), BF16),
+        ],
+        [
+            pltpu.VMEM((2 * rows, width), BF16),
+            pltpu.VMEM((width, width), BF16),
+            pltpu.SemaphoreType.DMA((2,)),
+            pltpu.SemaphoreType.DMA,
+        ],
+        1_000_000_000,
+        16,
+        pos, two_near, two_partner, dec_nbr, grid, dec_qkv,
+        scalars=1,
+        anywhere=(4, 5),
+        out_anywhere=(0,),
+    )
     (grid_out,) = call(
         decode_kernel,
         [((grid_rows, width), BF16)],
-        [((3 * rows, width), BF16)],
+        [],
         4_000_000_000,
-        pos, hidden_two, two_partner, two_off, dec_nbr, dec_queries, grid, dec_qkv, dec_out,
-        mlp_in, mlp_out,
-        scalars=1,
+        16,
+        two_off, off_picks, picked, dec_queries, grid_near, dec_qkv, dec_out, mlp_in, mlp_out,
     )
     return (grid_out, hidden_two)
 
@@ -250,7 +334,7 @@
     part = P(("groups", "nodes"), None)
     nodes = P("nodes", None)
     return jax.shard_map(
-        local,
+        step,
         mesh=mesh,
         in_specs=(part, part, nodes, nodes) + (P(),) * 8,
         out_specs=(part, part),

time: 56.3 us -> 47.9 us (0.85)
  local copies, waits for them, and re-layouts: 8.02 us -> 0.16 us
  starting transfers between devices: 26.4 us -> 25 us
  waiting for transfers between devices: 4.87 us -> 6.21 us
    unnamed x30 -> x21, local copies, waits for them, and re-layouts: 8.02 us -> 0.16 us
    ppermute x2, starting transfers between devices: 5.6 us -> 4.06 us  [exchange(): off = lax.ppermute(shard, 'nodes', outer_pairs)]
    ppermute x2, waiting for transfers between devices: 4.13 us -> 5.47 us  [exchange(): off = lax.ppermute(shard, 'nodes', outer_pairs)]
    pallas_call x5 -> x6, Pallas kernels: 15.8 us -> 15.6 us  [call(): pl.pallas_call(kernel, out_shape=[jax.ShapeDtypeStruct(shape, kind) for s...]
  transfers between devices with their start and end apart: 5 -> 5, of which waited for: 2 -> 3; matrix products, arithmetic and copies ran while one was open for 2% -> 0% of each run, Pallas kernels for 5% -> 11%
where the time goes in v2:
time: 47.9 us; the launch traced here: 47.8 us
  starting transfers between devices  25 us (52%)
  Pallas kernels  15.6 us (33%)
  waiting for transfers between devices  6.21 us (13%)
  between operations  0.81 us (2%)
    ppermute x2, starting transfers between devices, exchange(): return (lax.ppermute(shard, 'nodes', inner_pairs), off)  20.8 us
    pallas_call x6, Pallas kernels, call(): pl.pallas_call(kernel, out_shape=[jax.ShapeDtypeStruct(shape, kind) for s...  15.6 us
    ppermute x2, waiting for transfers between devices, exchange(): off = lax.ppermute(shard, 'nodes', outer_pairs)  5.47 us
    ppermute x2, starting transfers between devices, exchange(): off = lax.ppermute(shard, 'nodes', outer_pairs)  4.06 us
  transfers between devices with their start and end apart: 5, of which 3 were waited for; matrix products, arithmetic and copies ran while one was open for 0% of the time, Pallas kernels for 11%

profile of v2, /device:TPU:33, one launch (start us, length us, event | category | flops | bytes accessed | tf_op | source)
XLA Modules:
  0.0 47.8 jit_solution(605852967478860755)
XLA Ops:
  0.6 20.5 %collective-permute-start = (bf16[128,512]{1,0:T(8,128)(2,1)}, bf16[128,512]{1,0:T(8,128)(2,1)S(1)}, u32[]{:S(2)}, u32[]{:S(2)}) collective-permute-start(bf16[128,512]{1,0:T(8,128)(2,1)} %grid_hbm.3), channel_id=1, source_target_pairs={{0,1},{1,0},{2,3},{3,2},{4,5},{5,4},{6,7},{7,6},{8,9},{9,8},{10,11... | collective-permute-start | bytes 393224 | tf_op jit(solution)/shard_map/ppermute | solution.py:255
  21.2 1.9 %collective-permute-start.1 = (bf16[128,512]{1,0:T(8,128)(2,1)}, bf16[128,512]{1,0:T(8,128)(2,1)S(1)}, u32[]{:S(2)}, u32[]{:S(2)}) collective-permute-start(bf16[128,512]{1,0:T(8,128)(2,1)} %grid_hbm.3), channel_id=1, source_target_pairs={{1,2},{3,4},{5,6},{7,8},{9,10},{11,12},{13,14},{15,16},{17,18},{19... | collective-permute-start | bytes 393224 | tf_op jit(solution)/shard_map/ppermute | solution.py:254
  23.1 2.5 %shard_map.131 = (bf16[256,512]{1,0:T(8,128)(2,1)S(1)}, bf16[128,1024]{1,0:T(8,128)(2,1)S(1)}, f32[256,384]{1,0:T(8,128)S(1)}) custom-call(s32[1]{0:T(128)} %bitcast.pos_ref, bf16[128,512]{1,0:T(8,128)(2,1)} %grid_hbm.3, bf16[256,512]{1,0:T(8,128)(2,1)} %hidden_ref.1, s32[32,256]{1,0:T(8,128)} %bitcast.2, bf16[512,1536]{1,0:T(8,128)(2,1)} %qkv_ref.4), custom_call_target="tpu_custom_call" | custom-call | flops 2000000000 | tf_op jit(solution)/shard_map/pallas_call | solution.py:227
  25.6 0.0 collective-permute-done.partner_ref
  25.6 2.1 %collective-permute-done.1.off_ref = bf16[128,512]{1,0:T(8,128)(2,1)S(1)} collective-permute-done((bf16[128,512]{1,0:T(8,128)(2,1)}, bf16[128,512]{1,0:T(8,128)(2,1)S(1)}, u32[]{:S(2)}, u32[]{:S(2)}) %collective-permute-start.1) | collective-permute-done | bytes 131104 | tf_op jit(solution)/shard_map/ppermute | solution.py:254
  27.7 0.0 copy-done.5
  27.7 0.0 copy-start.3
  27.7 3.7 %shard_map.132.hidden_ref = bf16[256,512]{1,0:T(8,128)(2,1)S(1)} custom-call(bf16[256,512]{1,0:T(8,128)(2,1)S(1)} %get-tuple-element.12.queries_ref, bf16[128,1024]{1,0:T(8,128)(2,1)S(1)} %get-tuple-element.13.pairs_ref, f32[256,384]{1,0:T(8,128)S(1)} %get-tuple-element.14.bias_ref, bf16[128,512]{1,0:T(8,128)(2,1)S(1)} %collective-permute-done.partner_ref, ...), custom_call_target="tpu_custom_call" | custom-call | flops 4000000000 | tf_op jit(solution)/shard_map/pallas_call | solution.py:227
  31.4 0.0 copy-start.6
  31.4 0.1 collective-permute-start.2
  31.6 0.0 copy-done.3
  31.6 0.8 %shard_map.133 = (bf16[256,512]{1,0:T(8,128)(2,1)S(1)}, bf16[256,1024]{1,0:T(8,128)(2,1)S(1)}) custom-call(bf16[256,512]{1,0:T(8,128)(2,1)S(1)} %shard_map.132.hidden_ref, bf16[512,1536]{1,0:T(8,128)(2,1)S(1)} %copy-done.3), custom_call_target="tpu_custom_call" | custom-call | flops 1000000000 | tf_op jit(solution)/shard_map/pallas_call | solution.py:227
  32.4 0.7 %collective-permute-done.2.partner_ref = bf16[256,512]{1,0:T(8,128)(2,1)S(1)} collective-permute-done((bf16[256,512]{1,0:T(8,128)(2,1)S(1)}, bf16[256,512]{1,0:T(8,128)(2,1)S(1)}, u32[]{:S(2)}, u32[]{:S(2)}) %collective-permute-start.2) | collective-permute-done | bytes 262176 | tf_op jit(solution)/shard_map/ppermute | solution.py:282
  33.1 3.6 %shard_map.134.own_ref = bf16[256,512]{1,0:T(8,128)(2,1)S(1)} custom-call(bf16[256,512]{1,0:T(8,128)(2,1)S(1)} %get-tuple-element.15.queries_ref, bf16[256,1024]{1,0:T(8,128)(2,1)S(1)} %get-tuple-element.16.pairs_ref, bf16[256,512]{1,0:T(8,128)(2,1)S(1)} %shard_map.132.hidden_ref, bf16[256,512]{1,0:T(8,128)(2,1)S(1)} %collective-permute-done.2.partner_ref, ...), custom_call_target="tpu_custom_call" | custom-call | flops 4000000000 | tf_op jit(solution)/shard_map/pallas_call | solution.py:227
  36.7 0.3 collective-permute-start.4
  37.0 2.1 %collective-permute-start.3 = (bf16[256,512]{1,0:T(8,128)(2,1)S(1)}, bf16[256,512]{1,0:T(8,128)(2,1)S(1)}, u32[]{:S(2)}, u32[]{:S(2)}) collective-permute-start(bf16[256,512]{1,0:T(8,128)(2,1)S(1)} %shard_map.134.own_ref), channel_id=1, source_target_pairs={{1,2},{3,4},{5,6},{7,8},{9,10},{11,12},{13,14},{15,16},{17,18},{19... | collective-permute-start | bytes 786440 | tf_op jit(solution)/shard_map/ppermute | solution.py:254
  39.1 0.0 copy-done.9
  39.1 0.1 copy.14.nbr_ref
  39.2 0.0 copy-start.4
  39.2 0.0 collective-permute-done.4.partner_ref
  39.3 2.0 %shard_map.135 = (bf16[256,512]{1,0:T(8,128)(2,1)}, bf16[128,512]{1,0:T(8,128)(2,1)S(1)}, bf16[384,512]{1,0:T(8,128)(2,1)S(1)}, bf16[384,256]{1,0:T(8,128)(2,1)S(1)}, bf16[128,512]{1,0:T(8,128)(2,1)S(1)}) custom-call(s32[1]{0:T(128)} %bitcast.pos_ref, bf16[256,512]{1,0:T(8,128)(2,1)S(1)} %shard_map.134.own_ref, ...), custom_call_target="tpu_custom_call" | custom-call | flops 1000000000 | tf_op jit(solution)/shard_map/pallas_call | solution.py:227
  41.3 3.4 %collective-permute-done.3.off_ref = bf16[256,512]{1,0:T(8,128)(2,1)S(1)} collective-permute-done((bf16[256,512]{1,0:T(8,128)(2,1)S(1)}, bf16[256,512]{1,0:T(8,128)(2,1)S(1)}, u32[]{:S(2)}, u32[]{:S(2)}) %collective-permute-start.3) | collective-permute-done | bytes 262176 | tf_op jit(solution)/shard_map/ppermute | solution.py:254
  44.7 0.0 copy-done.4
  44.7 3.0 %shard_map.136 = bf16[128,512]{1,0:T(8,128)(2,1)} custom-call(bf16[256,512]{1,0:T(8,128)(2,1)S(1)} %collective-permute-done.3.off_ref, bf16[384,256]{1,0:T(8,128)(2,1)S(1)} %get-tuple-element.17.off_picks_ref, bf16[384,512]{1,0:T(8,128)(2,1)S(1)} %get-tuple-element.18.picked_ref, bf16[128,512]{1,0:T(8,128)(2,1)S(1)} %get-tuple-element.19.queries_ref, ...), custom_call_target="tpu_custom_call" | custom-call | flops 4000000000 | tf_op jit(solution)/shard_map/pallas_call | solution.py:227
  (13 shorter events, 0.0 us)
Async XLA Ops:
  0.6 25.0 %collective-permute-start = (bf16[128,512]{1,0:T(8,128)(2,1)}, bf16[128,512]{1,0:T(8,128)(2,1)S(1)}, u32[]{:S(2)}, u32[]{:S(2)}) collective-permute-start(bf16[128,512]{1,0:T(8,128)(2,1)} %grid_hbm.3), channel_id=1, source_target_pairs={{0,1},{1,0},{2,3},{3,2},{4,5},{5,4},{6,7},{7,6},{8,9},{9,8},{10,11... | collective-permute-start | bytes 393224 | tf_op jit(solution)/shard_map/ppermute | solution.py:255
  21.2 6.5 %collective-permute-start.1 = (bf16[128,512]{1,0:T(8,128)(2,1)}, bf16[128,512]{1,0:T(8,128)(2,1)S(1)}, u32[]{:S(2)}, u32[]{:S(2)}) collective-permute-start(bf16[128,512]{1,0:T(8,128)(2,1)} %grid_hbm.3), channel_id=1, source_target_pairs={{1,2},{3,4},{5,6},{7,8},{9,10},{11,12},{13,14},{15,16},{17,18},{19... | collective-permute-start | bytes 393224 | tf_op jit(solution)/shard_map/ppermute | solution.py:254
  23.1 4.6 %copy-start.2 = (bf16[512,1536]{1,0:T(8,128)(2,1)S(1)}, bf16[512,1536]{1,0:T(8,128)(2,1)}, u32[]{:S(2)}) copy-start(bf16[512,1536]{1,0:T(8,128)(2,1)} %qkv_ref.4) | copy-start | bytes 4718596
  23.1 4.6 %copy-start.5 = (bf16[512,512]{1,0:T(8,128)(2,1)S(1)}, bf16[512,512]{1,0:T(8,128)(2,1)}, u32[]{:S(2)}) copy-start(bf16[512,512]{1,0:T(8,128)(2,1)} %out_ref.3) | copy-start | bytes 1572868
  23.1 4.6 %copy-start.8 = (bf16[256,512]{1,0:T(8,128)(2,1)S(1)}, bf16[256,512]{1,0:T(8,128)(2,1)}, u32[]{:S(2)}) copy-start(bf16[256,512]{1,0:T(8,128)(2,1)} %hidden_ref.1) | copy-start | bytes 786436
  27.7 3.9 %copy-start.3 = (bf16[512,1536]{1,0:T(8,128)(2,1)S(1)}, bf16[512,1536]{1,0:T(8,128)(2,1)}, u32[]{:S(2)}) copy-start(bf16[512,1536]{1,0:T(8,128)(2,1)} %qkv_ref.6) | copy-start | bytes 4718596
  31.4 1.7 %copy-start.6 = (bf16[512,512]{1,0:T(8,128)(2,1)S(1)}, bf16[512,512]{1,0:T(8,128)(2,1)}, u32[]{:S(2)}) copy-start(bf16[512,512]{1,0:T(8,128)(2,1)} %out_ref.4) | copy-start | bytes 1572868
  31.4 1.7 %collective-permute-start.2 = (bf16[256,512]{1,0:T(8,128)(2,1)S(1)}, bf16[256,512]{1,0:T(8,128)(2,1)S(1)}, u32[]{:S(2)}, u32[]{:S(2)}) collective-permute-start(bf16[256,512]{1,0:T(8,128)(2,1)S(1)} %shard_map.132.hidden_ref), channel_id=1, source_target_pairs={{0,1},{1,0},{2,3},{3,2},{4,5},{5,4},{6,7},{7,6},{8,9},{9,8},{10,11... | collective-permute-start | bytes 786440 | tf_op jit(solution)/shard_map/ppermute | solution.py:282
  33.1 6.0 %copy-start.9 = (s32[128,3]{0,1:T(4,128)S(1)}, s32[128,3]{0,1:T(4,128)}, u32[]{:S(2)}) copy-start(s32[128,3]{0,1:T(4,128)} %param.15) | copy-start | bytes 4612
  33.1 11.6 %copy-start.1 = (bf16[2048,512]{1,0:T(8,128)(2,1)S(1)}, bf16[2048,512]{1,0:T(8,128)(2,1)}, u32[]{:S(2)}) copy-start(bf16[2048,512]{1,0:T(8,128)(2,1)} %mlp_out_ref.1) | copy-start | bytes 6291460
  33.1 11.6 %copy-start.7 = (bf16[512,512]{1,0:T(8,128)(2,1)S(1)}, bf16[512,512]{1,0:T(8,128)(2,1)}, u32[]{:S(2)}) copy-start(bf16[512,512]{1,0:T(8,128)(2,1)} %out_ref.5) | copy-start | bytes 1572868
  36.7 2.5 %collective-permute-start.4 = (bf16[256,512]{1,0:T(8,128)(2,1)S(1)}, bf16[256,512]{1,0:T(8,128)(2,1)S(1)}, u32[]{:S(2)}, u32[]{:S(2)}) collective-permute-start(bf16[256,512]{1,0:T(8,128)(2,1)S(1)} %shard_map.134.own_ref), channel_id=1, source_target_pairs={{0,1},{1,0},{2,3},{3,2},{4,5},{5,4},{6,7},{7,6},{8,9},{9,8},{10,11... | collective-permute-start | bytes 786440 | tf_op jit(solution)/shard_map/ppermute | solution.py:255
  37.0 7.7 %collective-permute-start.3 = (bf16[256,512]{1,0:T(8,128)(2,1)S(1)}, bf16[256,512]{1,0:T(8,128)(2,1)S(1)}, u32[]{:S(2)}, u32[]{:S(2)}) collective-permute-start(bf16[256,512]{1,0:T(8,128)(2,1)S(1)} %shard_map.134.own_ref), channel_id=1, source_target_pairs={{1,2},{3,4},{5,6},{7,8},{9,10},{11,12},{13,14},{15,16},{17,18},{19... | collective-permute-start | bytes 786440 | tf_op jit(solution)/shard_map/ppermute | solution.py:254
  39.2 5.5 %copy-start = (bf16[512,2048]{1,0:T(8,128)(2,1)S(1)}, bf16[512,2048]{1,0:T(8,128)(2,1)}, u32[]{:S(2)}) copy-start(bf16[512,2048]{1,0:T(8,128)(2,1)} %mlp_in_ref.1) | copy-start | bytes 6291460
  39.2 5.5 %copy-start.4 = (bf16[512,1536]{1,0:T(8,128)(2,1)S(1)}, bf16[512,1536]{1,0:T(8,128)(2,1)}, u32[]{:S(2)}) copy-start(bf16[512,1536]{1,0:T(8,128)(2,1)} %qkv_ref.7) | copy-start | bytes 4718596

commit v3 on v2

--- a/solution.py
+++ b/solution.py
@@ -7,9 +7,14 @@
 
 HEADS = 16
 LANES = 128
+ONES = 16
+CHUNK = 256
+DEPTH = 2
 EPSILON = 1e-05
 LOG2E = 1.4426950408889634
 MASKED = -1e30
+TINY = 2.0**-100
+HUGE = 2.0**100
 BF16 = jnp.bfloat16
 F32 = jnp.float32
 
@@ -27,10 +32,6 @@
 
 def dot_nt(left, right):
     return lax.dot_general(left, right, (((1,), (1,)), ((), ())), preferred_element_type=F32)
-
-
-def lane_head(shape, head_size):
-    return lax.broadcasted_iota(jnp.int32, shape, 1) // head_size
 
 
 def block_columns(lists, pos, odd, rows):
@@ -41,36 +42,93 @@
     return inside + jnp.where(block < 0, 2, block) * rows
 
 
-def attend(q_ref, kv_ref, mix_ref, bias_ref=None):
-    width = q_ref.shape[1]
+def keep_values(kept, values, first):
+    head_size = values.shape[1] // HEADS
+    count = values.shape[0]
+    turned = values.T
+    for h in range(HEADS):
+        kept[h, :head_size, first : first + count] = turned[h * head_size : (h + 1) * head_size]
+        kept[h, head_size:, first : first + count] = jnp.ones((ONES, count), BF16)
+
+
+def attend(q_ref, k_ref, kept, mix, counts_ref=None):
+    width = k_ref.shape[1]
     head_size = width // HEADS
-    keys = kv_ref.shape[0]
-    heads = lane_head((keys, LANES), head_size)
-    zero = jnp.zeros((keys, LANES), BF16)
-    one = jnp.ones((keys, LANES), BF16)
-    for t in range(width // LANES):
-        lanes = slice(t * LANES, (t + 1) * LANES)
-        queries = q_ref[:, lanes]
-        key_tile = kv_ref[:, lanes]
-        value_tile = kv_ref[:, width + t * LANES : width + (t + 1) * LANES]
-        total = None
-        for h in range(LANES // head_size):
-            chosen = heads == h
-            scores = dot_nt(queries, jnp.where(chosen, key_tile, zero))
-            if bias_ref is not None:
-                scores = scores + bias_ref[...]
-            weights = jnp.exp2(scores - jnp.max(scores, axis=1, keepdims=True)).astype(BF16)
-            values = jnp.concatenate(
-                [jnp.where(chosen, value_tile, zero), jnp.where(chosen, one, zero)], axis=1
-            )
-            part = dot(weights, values)
-            total = part if total is None else total + part
-        mix_ref[:, lanes] = (total[:, :LANES] / total[:, LANES:]).astype(BF16)
+    keys = k_ref.shape[0]
+    chunks = [slice(c, min(c + CHUNK, keys)) for c in range(0, keys, CHUNK)]
+    least = largest = None
+    waiting = []
+    for head in range(HEADS + DEPTH):
+        scores, mixed = [], None
+        tile = head * head_size // LANES * LANES
+        ready = waiting.pop(0) if head >= DEPTH else None
+        for i, chunk in enumerate(chunks):
+            if head < HEADS:
+                scores.append(dot(k_ref[chunk, tile : tile + LANES], q_ref[head]))
+            if ready is not None:
+                weights = jnp.exp2(ready[i]).astype(BF16)
+                if counts_ref is not None:
+                    weights = weights * counts_ref[chunk]
+                part = dot(kept[head - DEPTH, :, chunk], weights)
+                mixed = part if mixed is None else mixed + part
+        if head < HEADS:
+            waiting.append(scores)
+        if ready is not None:
+            total = mixed[head_size : head_size + 1]
+            first = (head - DEPTH) * head_size
+            mix[first : first + head_size] = (mixed[:head_size] / total).astype(BF16)
+            least = total if least is None else jnp.minimum(least, total)
+            largest = total if largest is None else jnp.maximum(largest, total)
+    return jnp.min(least), jnp.max(largest)
+
+
+def attend_exactly(q_ref, k_ref, kept, mix, counts_ref=None):
+    head_size = k_ref.shape[1] // HEADS
+
+    def one_head(head, carry):
+        tile = pl.multiple_of(head * head_size // LANES * LANES, LANES)
+        scores = dot(k_ref[:, pl.ds(tile, LANES)], q_ref[head])
+        if counts_ref is not None:
+            scores = jnp.where(counts_ref[...].astype(F32) > 0.0, scores, MASKED)
+        weights = jnp.exp2(scores - jnp.max(scores, axis=0, keepdims=True)).astype(BF16)
+        if counts_ref is not None:
+            weights = weights * counts_ref[...]
+        mixed = dot(kept[head], weights)
+        first = pl.multiple_of(head * head_size, head_size)
+        mix[pl.ds(first, head_size)] = (
+            mixed[:head_size] / mixed[head_size : head_size + 1]
+        ).astype(BF16)
+        return carry
+
+    lax.fori_loop(0, HEADS, one_head, 0)
+
+
+def attend_and_add(q_ref, k_ref, kept, mix, base_ref, out_ref, result_ref, counts_ref=None):
+    def finish():
+        added = dot(mix[...].T, out_ref[...])
+        result_ref[...] = (base_ref[...].astype(F32) + added).astype(BF16)
+
+    least, largest = attend(q_ref, k_ref, kept, mix, counts_ref)
+    finish()
+
+    @pl.when(jnp.logical_not(jnp.logical_and(least >= TINY, largest <= HUGE)))
+    def _():
+        attend_exactly(q_ref, k_ref, kept, mix, counts_ref)
+        finish()
+
+
+def spread_queries(target, queries):
+    head_size = queries.shape[1] // HEADS
+    turned = queries.T
+    for head in range(HEADS):
+        inside = head * head_size % LANES
+        target[head] = jnp.zeros(target.shape[1:], BF16)
+        target[head, inside : inside + head_size] = turned[head * head_size : (head + 1) * head_size]
 
 
 def prepare_kernel(
     pos_ref, grid_hbm, hidden_hbm, enc_nbr_hbm, enc_qkv_hbm,
-    queries_ref, pairs_ref, bias_ref,
+    queries_ref, pairs_ref, counts_ref,
     grid_ref, hidden_ref, enc_nbr_ref, enc_qkv_ref, arrived,
 ):
     width = grid_ref.shape[1]
@@ -89,59 +147,63 @@
     ]
     for copy in copies:
         copy.start()
+    copies[1].wait()
+    copies[2].wait()
+    normed = layer_norm(grid_ref[...])
+    normed_hidden = layer_norm(hidden_ref[...])
+    copies[3].wait()
     copies[0].wait()
+    pairs_ref[...] = dot(normed, enc_qkv_ref[:, width:]).astype(BF16)
+    queries = dot(normed_hidden, enc_qkv_ref[:, :width])
+    spread_queries(queries_ref, (queries * scale).astype(BF16))
     pos = pos_ref[0]
     columns = block_columns(enc_nbr_ref[...], pos, pos % 2, rows)
-    half = bias_ref.shape[1] // 2
+    half = counts_ref.shape[0] // 2
     columns = (columns - half).astype(F32).astype(BF16)
     one = jnp.ones((rows, columns.shape[1]), BF16)
-    for b in range(bias_ref.shape[1] // rows):
+    for b in range(counts_ref.shape[0] // rows):
         places = b * rows - half + lax.broadcasted_iota(jnp.int32, one.shape, 0)
         places = places.astype(F32).astype(BF16)
         counts = jnp.zeros_like(one)
         for k in range(columns.shape[0]):
             counts = counts + jnp.where(columns[k : k + 1] == places, one, jnp.zeros_like(one))
-        counts = counts.astype(F32)
-        bias = jnp.where(counts > 0.0, jnp.log2(jnp.maximum(counts, 1.0)), MASKED)
-        bias_ref[:, b * rows : (b + 1) * rows] = bias.T
-    copies[1].wait()
-    copies[2].wait()
-    normed = layer_norm(grid_ref[...])
-    normed_hidden = layer_norm(hidden_ref[...])
-    copies[3].wait()
-    pairs_ref[...] = dot(normed, enc_qkv_ref[:, width:]).astype(BF16)
-    queries = dot(normed_hidden, enc_qkv_ref[:, :width])
-    queries_ref[...] = (queries * scale).astype(BF16)
+        counts_ref[b * rows : (b + 1) * rows] = counts
 
 
 def encode_kernel(
-    queries_ref, pairs_ref, bias_ref, partner_ref, off_ref, hidden_ref, qkv_ref, out_ref,
-    result_ref, pairs, mix,
+    queries_ref, pairs_ref, counts_ref, partner_ref, off_ref, hidden_ref, qkv_ref, out_ref,
+    result_ref, keys, kept, mix,
 ):
     width = hidden_ref.shape[1]
     rows = pairs_ref.shape[0]
-    pairs[:rows] = pairs_ref[...]
+    keys[:rows] = pairs_ref[:, :width]
+    keep_values(kept, pairs_ref[:, width:], 0)
     normed = jnp.concatenate([layer_norm(partner_ref[...]), layer_norm(off_ref[...])], axis=0)
-    pairs[rows:] = dot(normed, qkv_ref[:, width:]).astype(BF16)
-    attend(queries_ref, pairs, mix, bias_ref)
-    result_ref[...] = (hidden_ref[...].astype(F32) + dot(mix[...], out_ref[...])).astype(BF16)
+    pairs = dot(normed, qkv_ref[:, width:]).astype(BF16)
+    keys[rows:] = pairs[:, :width]
+    keep_values(kept, pairs[:, width:], rows)
+    attend_and_add(queries_ref, keys, kept, mix, hidden_ref, out_ref, result_ref, counts_ref)
 
 
 def project_kernel(hidden_ref, qkv_ref, queries_ref, pairs_ref):
     width = hidden_ref.shape[1]
     scale = LOG2E / (width // HEADS) ** 0.5
     normed = layer_norm(hidden_ref[...])
-    queries_ref[...] = (dot(normed, qkv_ref[:, :width]) * scale).astype(BF16)
+    spread_queries(queries_ref, (dot(normed, qkv_ref[:, :width]) * scale).astype(BF16))
     pairs_ref[...] = dot(normed, qkv_ref[:, width:]).astype(BF16)
 
 
-def process_kernel(queries_ref, pairs_ref, hidden_ref, partner_ref, qkv_ref, out_ref, result_ref, pairs, mix):
+def process_kernel(
+    queries_ref, pairs_ref, hidden_ref, partner_ref, qkv_ref, out_ref, result_ref, keys, kept, mix
+):
     width = hidden_ref.shape[1]
     rows = hidden_ref.shape[0]
-    pairs[:rows] = pairs_ref[...]
-    pairs[rows:] = dot(layer_norm(partner_ref[...]), qkv_ref[:, width:]).astype(BF16)
-    attend(queries_ref, pairs, mix)
-    result_ref[...] = (hidden_ref[...].astype(F32) + dot(mix[...], out_ref[...])).astype(BF16)
+    keys[:rows] = pairs_ref[:, :width]
+    keep_values(kept, pairs_ref[:, width:], 0)
+    pairs = dot(layer_norm(partner_ref[...]), qkv_ref[:, width:]).astype(BF16)
+    keys[rows:] = pairs[:, :width]
+    keep_values(kept, pairs[:, width:], rows)
+    attend_and_add(queries_ref, keys, kept, mix, hidden_ref, out_ref, result_ref)
 
 
 def picks_of(columns, first, rows):
@@ -237,6 +299,14 @@
     )(*args)
 
 
+def attention_scratch(keys, rows, width):
+    return [
+        pltpu.VMEM((keys, width), BF16),
+        pltpu.VMEM((HEADS, width // HEADS + ONES, keys), BF16),
+        pltpu.VMEM((width, rows), BF16),
+    ]
+
+
 def step(
     grid, hidden, enc_nbr, dec_nbr, enc_qkv, enc_out, proc_qkv, proc_out, dec_qkv, dec_out,
     mlp_in, mlp_out,
@@ -255,9 +325,9 @@
         return lax.ppermute(shard, "nodes", inner_pairs), off
 
     grid_partner, grid_off = exchange(grid)
-    queries, pairs, bias = call(
+    queries, pairs, counts = call(
         prepare_kernel,
-        [((rows, width), BF16), ((grid_rows, 2 * width), BF16), ((rows, 3 * grid_rows), F32)],
+        [((HEADS, LANES, rows), BF16), ((grid_rows, 2 * width), BF16), ((3 * grid_rows, rows), BF16)],
         [
             pltpu.VMEM(grid.shape, BF16),
             pltpu.VMEM(hidden.shape, BF16),
@@ -274,15 +344,15 @@
     (hidden_one,) = call(
         encode_kernel,
         [((rows, width), BF16)],
-        [pltpu.VMEM((3 * grid_rows, 2 * width), BF16), pltpu.VMEM((rows, width), BF16)],
+        attention_scratch(3 * grid_rows, rows, width),
         4_000_000_000,
         16,
-        queries, pairs, bias, grid_partner, grid_off, hidden, enc_qkv, enc_out,
+        queries, pairs, counts, grid_partner, grid_off, hidden, enc_qkv, enc_out,
     )
     one_partner = lax.ppermute(hidden_one, "nodes", inner_pairs)
     queries, pairs = call(
         project_kernel,
-        [((rows, width), BF16), ((rows, 2 * width), BF16)],
+        [((HEADS, LANES, rows), BF16), ((rows, 2 * width), BF16)],
         [],
         1_000_000_000,
         16,
@@ -291,7 +361,7 @@
     (two_near,) = call(
         process_kernel,
         [((rows, width), BF16)],
-        [pltpu.VMEM((2 * rows, 2 * width), BF16), pltpu.VMEM((rows, width), BF16)],
+        attention_scratch(2 * rows, rows, width),
         4_000_000_000,
         16,
         queries, pairs, hidden_one, one_partner, proc_qkv, proc_out,

time: 47.9 us -> 45.5 us (0.950)
  Pallas kernels: 15.6 us -> 13.5 us
    pallas_call x6, Pallas kernels: 15.6 us -> 13.5 us  [call(): pl.pallas_call(kernel, out_shape=[jax.ShapeDtypeStruct(shape, kind) for s...]
  transfers between devices with their start and end apart: 5 -> 5, of which waited for: 3 -> 3; matrix products, arithmetic and copies ran while one was open for 0% -> 0% of each run, Pallas kernels for 11% -> 12%
where the time goes in v3:
time: 45.5 us; the launch traced here: 45.3 us
  starting transfers between devices  24.8 us (55%)
  Pallas kernels  13.5 us (30%)
  waiting for transfers between devices  6.08 us (13%)
  between operations  0.79 us (2%)
    ppermute x2, starting transfers between devices, exchange(): return (lax.ppermute(shard, 'nodes', inner_pairs), off)  20.8 us
    pallas_call x6, Pallas kernels, call(): pl.pallas_call(kernel, out_shape=[jax.ShapeDtypeStruct(shape, kind) for s...  13.5 us
    ppermute x2, waiting for transfers between devices, exchange(): off = lax.ppermute(shard, 'nodes', outer_pairs)  5.36 us
    ppermute x2, starting transfers between devices, exchange(): off = lax.ppermute(shard, 'nodes', outer_pairs)  3.88 us
  transfers between devices with their start and end apart: 5, of which 3 were waited for; matrix products, arithmetic and copies ran while one was open for 0% of the time, Pallas kernels for 12%

profile of v3, /device:TPU:33, one launch (start us, length us, event | category | flops | bytes accessed | tf_op | source)
XLA Modules:
  0.0 45.3 jit_solution(12209429416817936815)
XLA Ops:
  0.6 20.5 %collective-permute-start = (bf16[128,512]{1,0:T(8,128)(2,1)}, bf16[128,512]{1,0:T(8,128)(2,1)S(1)}, u32[]{:S(2)}, u32[]{:S(2)}) collective-permute-start(bf16[128,512]{1,0:T(8,128)(2,1)} %grid_hbm.3), channel_id=1, source_target_pairs={{0,1},{1,0},{2,3},{3,2},{4,5},{5,4},{6,7},{7,6},{8,9},{9,8},{10,11... | collective-permute-start | bytes 393224 | tf_op jit(solution)/shard_map/ppermute | solution.py:325
  21.2 1.9 %collective-permute-start.1 = (bf16[128,512]{1,0:T(8,128)(2,1)}, bf16[128,512]{1,0:T(8,128)(2,1)S(1)}, u32[]{:S(2)}, u32[]{:S(2)}) collective-permute-start(bf16[128,512]{1,0:T(8,128)(2,1)} %grid_hbm.3), channel_id=1, source_target_pairs={{1,2},{3,4},{5,6},{7,8},{9,10},{11,12},{13,14},{15,16},{17,18},{19... | collective-permute-start | bytes 393224 | tf_op jit(solution)/shard_map/ppermute | solution.py:324
  23.1 0.0 copy-start.2
  23.1 2.8 %shard_map.131 = (bf16[16,128,256]{2,1,0:T(8,128)(2,1)S(1)}, bf16[128,1024]{1,0:T(8,128)(2,1)S(1)}, bf16[384,256]{1,0:T(8,128)(2,1)S(1)}) custom-call(s32[1]{0:T(128)} %bitcast.pos_ref, bf16[128,512]{1,0:T(8,128)(2,1)} %grid_hbm.3, bf16[256,512]{1,0:T(8,128)(2,1)} %hidden_ref.1, s32[32,256]{1,0:T(8,128)} %bitcast.2, bf16[512,1536]{1,0:T(8,128)(2,1)} %qkv_ref.4), custom_call_target="tpu_custom_call" | custom-call | flops 2000000000 | tf_op jit(solution)/shard_map/pallas_call | solution.py:289
  25.9 0.0 collective-permute-done.partner_ref
  25.9 1.8 %collective-permute-done.1.off_ref = bf16[128,512]{1,0:T(8,128)(2,1)S(1)} collective-permute-done((bf16[128,512]{1,0:T(8,128)(2,1)}, bf16[128,512]{1,0:T(8,128)(2,1)S(1)}, u32[]{:S(2)}, u32[]{:S(2)}) %collective-permute-start.1) | collective-permute-done | bytes 131104 | tf_op jit(solution)/shard_map/ppermute | solution.py:324
  27.7 0.0 copy-done.5
  27.7 0.0 copy-start.3
  27.7 2.4 %shard_map.132.hidden_ref = bf16[256,512]{1,0:T(8,128)(2,1)S(1)} custom-call(bf16[16,128,256]{2,1,0:T(8,128)(2,1)S(1)} %get-tuple-element.12.queries_ref, bf16[128,1024]{1,0:T(8,128)(2,1)S(1)} %get-tuple-element.13.pairs_ref, bf16[384,256]{1,0:T(8,128)(2,1)S(1)} %get-tuple-element.14.counts_ref, bf16[128,512]{1,0:T(8,128)(2,1)S(1)} %collective-permute-done.partner_ref, ...), custom_call_target="tpu_custom_call" | custom-call | flops 4000000000 | tf_op jit(solution)/shard_map/pallas_call | solution.py:289
  30.1 0.0 copy-start.6
  30.1 0.1 collective-permute-start.2
  30.2 0.8 %shard_map.133 = (bf16[16,128,256]{2,1,0:T(8,128)(2,1)S(1)}, bf16[256,1024]{1,0:T(8,128)(2,1)S(1)}) custom-call(bf16[256,512]{1,0:T(8,128)(2,1)S(1)} %shard_map.132.hidden_ref, bf16[512,1536]{1,0:T(8,128)(2,1)S(1)} %copy-done.3), custom_call_target="tpu_custom_call" | custom-call | flops 1000000000 | tf_op jit(solution)/shard_map/pallas_call | solution.py:289
  31.0 0.7 %collective-permute-done.2.partner_ref = bf16[256,512]{1,0:T(8,128)(2,1)S(1)} collective-permute-done((bf16[256,512]{1,0:T(8,128)(2,1)S(1)}, bf16[256,512]{1,0:T(8,128)(2,1)S(1)}, u32[]{:S(2)}, u32[]{:S(2)}) %collective-permute-start.2) | collective-permute-done | bytes 262176 | tf_op jit(solution)/shard_map/ppermute | solution.py:352
  31.7 0.0 copy-done.6
  31.8 2.6 %shard_map.134.own_ref = bf16[256,512]{1,0:T(8,128)(2,1)S(1)} custom-call(bf16[16,128,256]{2,1,0:T(8,128)(2,1)S(1)} %get-tuple-element.15.queries_ref, bf16[256,1024]{1,0:T(8,128)(2,1)S(1)} %get-tuple-element.16.pairs_ref, bf16[256,512]{1,0:T(8,128)(2,1)S(1)} %shard_map.132.hidden_ref, bf16[256,512]{1,0:T(8,128)(2,1)S(1)} %collective-permute-done.2.partner_ref, ...), custom_call_target="tpu_custom_call" | custom-call | flops 4000000000 | tf_op jit(solution)/shard_map/pallas_call | solution.py:289
  34.3 0.3 collective-permute-start.4
  34.6 1.9 %collective-permute-start.3 = (bf16[256,512]{1,0:T(8,128)(2,1)S(1)}, bf16[256,512]{1,0:T(8,128)(2,1)S(1)}, u32[]{:S(2)}, u32[]{:S(2)}) collective-permute-start(bf16[256,512]{1,0:T(8,128)(2,1)S(1)} %shard_map.134.own_ref), channel_id=1, source_target_pairs={{1,2},{3,4},{5,6},{7,8},{9,10},{11,12},{13,14},{15,16},{17,18},{19... | collective-permute-start | bytes 786440 | tf_op jit(solution)/shard_map/ppermute | solution.py:324
  36.5 0.1 copy.14.nbr_ref
  36.6 0.0 copy-start.4
  36.7 0.0 collective-permute-done.4.partner_ref
  36.7 2.0 %shard_map.135 = (bf16[256,512]{1,0:T(8,128)(2,1)}, bf16[128,512]{1,0:T(8,128)(2,1)S(1)}, bf16[384,512]{1,0:T(8,128)(2,1)S(1)}, bf16[384,256]{1,0:T(8,128)(2,1)S(1)}, bf16[128,512]{1,0:T(8,128)(2,1)S(1)}) custom-call(s32[1]{0:T(128)} %bitcast.pos_ref, bf16[256,512]{1,0:T(8,128)(2,1)S(1)} %shard_map.134.own_ref, ...), custom_call_target="tpu_custom_call" | custom-call | flops 1000000000 | tf_op jit(solution)/shard_map/pallas_call | solution.py:289
  38.7 3.6 %collective-permute-done.3.off_ref = bf16[256,512]{1,0:T(8,128)(2,1)S(1)} collective-permute-done((bf16[256,512]{1,0:T(8,128)(2,1)S(1)}, bf16[256,512]{1,0:T(8,128)(2,1)S(1)}, u32[]{:S(2)}, u32[]{:S(2)}) %collective-permute-start.3) | collective-permute-done | bytes 262176 | tf_op jit(solution)/shard_map/ppermute | solution.py:324
  42.3 0.0 copy-done.4
  42.3 3.0 %shard_map.136 = bf16[128,512]{1,0:T(8,128)(2,1)} custom-call(bf16[256,512]{1,0:T(8,128)(2,1)S(1)} %collective-permute-done.3.off_ref, bf16[384,256]{1,0:T(8,128)(2,1)S(1)} %get-tuple-element.17.off_picks_ref, bf16[384,512]{1,0:T(8,128)(2,1)S(1)} %get-tuple-element.18.picked_ref, bf16[128,512]{1,0:T(8,128)(2,1)S(1)} %get-tuple-element.19.queries_ref, ...), custom_call_target="tpu_custom_call" | custom-call | flops 4000000000 | tf_op jit(solution)/shard_map/pallas_call | solution.py:289
  (13 shorter events, 0.0 us)
Async XLA Ops:
  0.6 25.3 %collective-permute-start = (bf16[128,512]{1,0:T(8,128)(2,1)}, bf16[128,512]{1,0:T(8,128)(2,1)S(1)}, u32[]{:S(2)}, u32[]{:S(2)}) collective-permute-start(bf16[128,512]{1,0:T(8,128)(2,1)} %grid_hbm.3), channel_id=1, source_target_pairs={{0,1},{1,0},{2,3},{3,2},{4,5},{5,4},{6,7},{7,6},{8,9},{9,8},{10,11... | collective-permute-start | bytes 393224 | tf_op jit(solution)/shard_map/ppermute | solution.py:325
  21.2 6.5 %collective-permute-start.1 = (bf16[128,512]{1,0:T(8,128)(2,1)}, bf16[128,512]{1,0:T(8,128)(2,1)S(1)}, u32[]{:S(2)}, u32[]{:S(2)}) collective-permute-start(bf16[128,512]{1,0:T(8,128)(2,1)} %grid_hbm.3), channel_id=1, source_target_pairs={{1,2},{3,4},{5,6},{7,8},{9,10},{11,12},{13,14},{15,16},{17,18},{19... | collective-permute-start | bytes 393224 | tf_op jit(solution)/shard_map/ppermute | solution.py:324
  23.1 4.6 %copy-start.2 = (bf16[512,1536]{1,0:T(8,128)(2,1)S(1)}, bf16[512,1536]{1,0:T(8,128)(2,1)}, u32[]{:S(2)}) copy-start(bf16[512,1536]{1,0:T(8,128)(2,1)} %qkv_ref.4) | copy-start | bytes 4718596
  23.1 4.6 %copy-start.5 = (bf16[512,512]{1,0:T(8,128)(2,1)S(1)}, bf16[512,512]{1,0:T(8,128)(2,1)}, u32[]{:S(2)}) copy-start(bf16[512,512]{1,0:T(8,128)(2,1)} %out_ref.3) | copy-start | bytes 1572868
  23.1 4.6 %copy-start.8 = (bf16[256,512]{1,0:T(8,128)(2,1)S(1)}, bf16[256,512]{1,0:T(8,128)(2,1)}, u32[]{:S(2)}) copy-start(bf16[256,512]{1,0:T(8,128)(2,1)} %hidden_ref.1) | copy-start | bytes 786436
  27.7 2.5 %copy-start.3 = (bf16[512,1536]{1,0:T(8,128)(2,1)S(1)}, bf16[512,1536]{1,0:T(8,128)(2,1)}, u32[]{:S(2)}) copy-start(bf16[512,1536]{1,0:T(8,128)(2,1)} %qkv_ref.6) | copy-start | bytes 4718596
  30.1 1.7 %copy-start.6 = (bf16[512,512]{1,0:T(8,128)(2,1)S(1)}, bf16[512,512]{1,0:T(8,128)(2,1)}, u32[]{:S(2)}) copy-start(bf16[512,512]{1,0:T(8,128)(2,1)} %out_ref.4) | copy-start | bytes 1572868
  30.1 1.7 %collective-permute-start.2 = (bf16[256,512]{1,0:T(8,128)(2,1)S(1)}, bf16[256,512]{1,0:T(8,128)(2,1)S(1)}, u32[]{:S(2)}, u32[]{:S(2)}) collective-permute-start(bf16[256,512]{1,0:T(8,128)(2,1)S(1)} %shard_map.132.hidden_ref), channel_id=1, source_target_pairs={{0,1},{1,0},{2,3},{3,2},{4,5},{5,4},{6,7},{7,6},{8,9},{9,8},{10,11... | collective-permute-start | bytes 786440 | tf_op jit(solution)/shard_map/ppermute | solution.py:352
  31.7 4.8 %copy-start.9 = (s32[128,3]{0,1:T(4,128)S(1)}, s32[128,3]{0,1:T(4,128)}, u32[]{:S(2)}) copy-start(s32[128,3]{0,1:T(4,128)} %param.15) | copy-start | bytes 4612
  31.7 10.5 %copy-start.1 = (bf16[2048,512]{1,0:T(8,128)(2,1)S(1)}, bf16[2048,512]{1,0:T(8,128)(2,1)}, u32[]{:S(2)}) copy-start(bf16[2048,512]{1,0:T(8,128)(2,1)} %mlp_out_ref.1) | copy-start | bytes 6291460
  31.7 10.5 %copy-start.7 = (bf16[512,512]{1,0:T(8,128)(2,1)S(1)}, bf16[512,512]{1,0:T(8,128)(2,1)}, u32[]{:S(2)}) copy-start(bf16[512,512]{1,0:T(8,128)(2,1)} %out_ref.5) | copy-start | bytes 1572868
  34.3 2.3 %collective-permute-start.4 = (bf16[256,512]{1,0:T(8,128)(2,1)S(1)}, bf16[256,512]{1,0:T(8,128)(2,1)S(1)}, u32[]{:S(2)}, u32[]{:S(2)}) collective-permute-start(bf16[256,512]{1,0:T(8,128)(2,1)S(1)} %shard_map.134.own_ref), channel_id=1, source_target_pairs={{0,1},{1,0},{2,3},{3,2},{4,5},{5,4},{6,7},{7,6},{8,9},{9,8},{10,11... | collective-permute-start | bytes 786440 | tf_op jit(solution)/shard_map/ppermute | solution.py:325
  34.6 7.7 %collective-permute-start.3 = (bf16[256,512]{1,0:T(8,128)(2,1)S(1)}, bf16[256,512]{1,0:T(8,128)(2,1)S(1)}, u32[]{:S(2)}, u32[]{:S(2)}) collective-permute-start(bf16[256,512]{1,0:T(8,128)(2,1)S(1)} %shard_map.134.own_ref), channel_id=1, source_target_pairs={{1,2},{3,4},{5,6},{7,8},{9,10},{11,12},{13,14},{15,16},{17,18},{19... | collective-permute-start | bytes 786440 | tf_op jit(solution)/shard_map/ppermute | solution.py:324
  36.6 5.6 %copy-start = (bf16[512,2048]{1,0:T(8,128)(2,1)S(1)}, bf16[512,2048]{1,0:T(8,128)(2,1)}, u32[]{:S(2)}) copy-start(bf16[512,2048]{1,0:T(8,128)(2,1)} %mlp_in_ref.1) | copy-start | bytes 6291460
  36.6 5.6 %copy-start.4 = (bf16[512,1536]{1,0:T(8,128)(2,1)S(1)}, bf16[512,1536]{1,0:T(8,128)(2,1)}, u32[]{:S(2)}) copy-start(bf16[512,1536]{1,0:T(8,128)(2,1)} %qkv_ref.7) | copy-start | bytes 4718596

commit v4 on v3

--- a/solution.py
+++ b/solution.py
@@ -1,3 +1,5 @@
+import functools
+
 import jax
 import jax.numpy as jnp
 from jax import lax
@@ -51,12 +53,11 @@
         kept[h, head_size:, first : first + count] = jnp.ones((ONES, count), BF16)
 
 
-def attend(q_ref, k_ref, kept, mix, counts_ref=None):
+def weigh(q_ref, k_ref, kept, consume, counts_ref=None):
     width = k_ref.shape[1]
     head_size = width // HEADS
     keys = k_ref.shape[0]
     chunks = [slice(c, min(c + CHUNK, keys)) for c in range(0, keys, CHUNK)]
-    least = largest = None
     waiting = []
     for head in range(HEADS + DEPTH):
         scores, mixed = [], None
@@ -74,12 +75,7 @@
         if head < HEADS:
             waiting.append(scores)
         if ready is not None:
-            total = mixed[head_size : head_size + 1]
-            first = (head - DEPTH) * head_size
-            mix[first : first + head_size] = (mixed[:head_size] / total).astype(BF16)
-            least = total if least is None else jnp.minimum(least, total)
-            largest = total if largest is None else jnp.maximum(largest, total)
-    return jnp.min(least), jnp.max(largest)
+            consume(head - DEPTH, mixed)
 
 
 def attend_exactly(q_ref, k_ref, kept, mix, counts_ref=None):
@@ -103,18 +99,39 @@
     lax.fori_loop(0, HEADS, one_head, 0)
 
 
-def attend_and_add(q_ref, k_ref, kept, mix, base_ref, out_ref, result_ref, counts_ref=None):
+def attend_and_add(
+    q_ref, k_ref, kept, mix, base_ref, out_ref, result_ref, exactly, counts_ref=None, sums_ref=None
+):
+    head_size = k_ref.shape[1] // HEADS
+    totals = []
+
+    def consume(head, mixed):
+        if sums_ref is not None:
+            mixed = mixed + sums_ref[head]
+        total = mixed[head_size : head_size + 1]
+        totals.append(total)
+        mix[head * head_size : (head + 1) * head_size] = (mixed[:head_size] / total).astype(BF16)
+
     def finish():
         added = dot(mix[...].T, out_ref[...])
         result_ref[...] = (base_ref[...].astype(F32) + added).astype(BF16)
 
-    least, largest = attend(q_ref, k_ref, kept, mix, counts_ref)
+    weigh(q_ref, k_ref, kept, consume, counts_ref)
+    least = largest = totals[0]
+    for total in totals[1:]:
+        least, largest = jnp.minimum(least, total), jnp.maximum(largest, total)
+    least, largest = jnp.min(least), jnp.max(largest)
     finish()
 
     @pl.when(jnp.logical_not(jnp.logical_and(least >= TINY, largest <= HUGE)))
     def _():
-        attend_exactly(q_ref, k_ref, kept, mix, counts_ref)
+        exactly()
         finish()
+
+
+def clear_queries(target):
+    for head in range(HEADS):
+        target[head] = jnp.zeros(target.shape[1:], BF16)
 
 
 def spread_queries(target, queries):
@@ -122,14 +139,13 @@
     turned = queries.T
     for head in range(HEADS):
         inside = head * head_size % LANES
-        target[head] = jnp.zeros(target.shape[1:], BF16)
         target[head, inside : inside + head_size] = turned[head * head_size : (head + 1) * head_size]
 
 
 def prepare_kernel(
     pos_ref, grid_hbm, hidden_hbm, enc_nbr_hbm, enc_qkv_hbm,
-    queries_ref, pairs_ref, counts_ref,
-    grid_ref, hidden_ref, enc_nbr_ref, enc_qkv_ref, arrived,
+    queries_ref, pairs_ref, counts_ref, hidden_ref, pair_weights,
+    grid_ref, enc_nbr_ref, query_weights, arrived,
 ):
     width = grid_ref.shape[1]
     rows = grid_ref.shape[0]
@@ -139,23 +155,17 @@
         for i, (source, target) in enumerate(
             [
                 (enc_nbr_hbm, enc_nbr_ref),
+                (hidden_hbm, hidden_ref),
                 (grid_hbm, grid_ref),
-                (hidden_hbm, hidden_ref),
-                (enc_qkv_hbm, enc_qkv_ref),
+                (enc_qkv_hbm.at[:, :width], query_weights),
+                (enc_qkv_hbm.at[:, width:], pair_weights),
             ]
         )
     ]
     for copy in copies:
         copy.start()
-    copies[1].wait()
-    copies[2].wait()
-    normed = layer_norm(grid_ref[...])
-    normed_hidden = layer_norm(hidden_ref[...])
-    copies[3].wait()
+    clear_queries(queries_ref)
     copies[0].wait()
-    pairs_ref[...] = dot(normed, enc_qkv_ref[:, width:]).astype(BF16)
-    queries = dot(normed_hidden, enc_qkv_ref[:, :width])
-    spread_queries(queries_ref, (queries * scale).astype(BF16))
     pos = pos_ref[0]
     columns = block_columns(enc_nbr_ref[...], pos, pos % 2, rows)
     half = counts_ref.shape[0] // 2
@@ -168,10 +178,15 @@
         for k in range(columns.shape[0]):
             counts = counts + jnp.where(columns[k : k + 1] == places, one, jnp.zeros_like(one))
         counts_ref[b * rows : (b + 1) * rows] = counts
+    for copy in copies[1:]:
+        copy.wait()
+    queries = dot(layer_norm(hidden_ref[...]), query_weights[...])
+    spread_queries(queries_ref, (queries * scale).astype(BF16))
+    pairs_ref[...] = dot(layer_norm(grid_ref[...]), pair_weights[...]).astype(BF16)
 
 
 def encode_kernel(
-    queries_ref, pairs_ref, counts_ref, partner_ref, off_ref, hidden_ref, qkv_ref, out_ref,
+    queries_ref, pairs_ref, counts_ref, partner_ref, off_ref, hidden_ref, pair_weights, out_ref,
     result_ref, keys, kept, mix,
 ):
     width = hidden_ref.shape[1]
@@ -179,31 +194,51 @@
     keys[:rows] = pairs_ref[:, :width]
     keep_values(kept, pairs_ref[:, width:], 0)
     normed = jnp.concatenate([layer_norm(partner_ref[...]), layer_norm(off_ref[...])], axis=0)
-    pairs = dot(normed, qkv_ref[:, width:]).astype(BF16)
+    pairs = dot(normed, pair_weights[...]).astype(BF16)
     keys[rows:] = pairs[:, :width]
     keep_values(kept, pairs[:, width:], rows)
-    attend_and_add(queries_ref, keys, kept, mix, hidden_ref, out_ref, result_ref, counts_ref)
-
-
-def project_kernel(hidden_ref, qkv_ref, queries_ref, pairs_ref):
+    exactly = functools.partial(attend_exactly, queries_ref, keys, kept, mix, counts_ref)
+    attend_and_add(
+        queries_ref, keys, kept, mix, hidden_ref, out_ref, result_ref, exactly, counts_ref
+    )
+
+
+def project_kernel(hidden_ref, qkv_ref, queries_ref, keys, kept, sums_ref):
     width = hidden_ref.shape[1]
     scale = LOG2E / (width // HEADS) ** 0.5
+    clear_queries(queries_ref)
     normed = layer_norm(hidden_ref[...])
     spread_queries(queries_ref, (dot(normed, qkv_ref[:, :width]) * scale).astype(BF16))
-    pairs_ref[...] = dot(normed, qkv_ref[:, width:]).astype(BF16)
+    pairs = dot(normed, qkv_ref[:, width:]).astype(BF16)
+    keys[...] = pairs[:, :width]
+    keep_values(kept, pairs[:, width:], 0)
+
+    def consume(head, mixed):
+        sums_ref[head] = mixed
+
+    weigh(queries_ref, keys, kept, consume)
 
 
 def process_kernel(
-    queries_ref, pairs_ref, hidden_ref, partner_ref, qkv_ref, out_ref, result_ref, keys, kept, mix
+    queries_ref, own_keys, own_kept, sums_ref, hidden_ref, partner_ref, qkv_ref, out_ref,
+    result_ref, keys, kept, mix, all_keys, all_kept,
 ):
     width = hidden_ref.shape[1]
     rows = hidden_ref.shape[0]
-    keys[:rows] = pairs_ref[:, :width]
-    keep_values(kept, pairs_ref[:, width:], 0)
     pairs = dot(layer_norm(partner_ref[...]), qkv_ref[:, width:]).astype(BF16)
-    keys[rows:] = pairs[:, :width]
-    keep_values(kept, pairs[:, width:], rows)
-    attend_and_add(queries_ref, keys, kept, mix, hidden_ref, out_ref, result_ref)
+    keys[...] = pairs[:, :width]
+    keep_values(kept, pairs[:, width:], 0)
+
+    def exactly():
+        all_keys[:rows] = own_keys[...]
+        all_keys[rows:] = keys[...]
+        all_kept[:, :, :rows] = own_kept[...]
+        all_kept[:, :, rows:] = kept[...]
+        attend_exactly(queries_ref, all_keys, all_kept, mix)
+
+    attend_and_add(
+        queries_ref, keys, kept, mix, hidden_ref, out_ref, result_ref, exactly, sums_ref=sums_ref
+    )
 
 
 def picks_of(columns, first, rows):
@@ -299,11 +334,10 @@
     )(*args)
 
 
-def attention_scratch(keys, rows, width):
+def attention_scratch(keys, width):
     return [
         pltpu.VMEM((keys, width), BF16),
         pltpu.VMEM((HEADS, width // HEADS + ONES, keys), BF16),
-        pltpu.VMEM((width, rows), BF16),
     ]
 
 
@@ -325,15 +359,21 @@
         return lax.ppermute(shard, "nodes", inner_pairs), off
 
     grid_partner, grid_off = exchange(grid)
-    queries, pairs, counts = call(
+    kept_rows = width // HEADS + ONES
+    queries, pairs, counts, hidden_near, pair_weights = call(
         prepare_kernel,
-        [((HEADS, LANES, rows), BF16), ((grid_rows, 2 * width), BF16), ((3 * grid_rows, rows), BF16)],
+        [
+            ((HEADS, LANES, rows), BF16),
+            ((grid_rows, 2 * width), BF16),
+            ((3 * grid_rows, rows), BF16),
+            ((rows, width), BF16),
+            ((width, 2 * width), BF16),
+        ],
         [
             pltpu.VMEM(grid.shape, BF16),
-            pltpu.VMEM(hidden.shape, BF16),
             pltpu.VMEM(enc_nbr.shape[::-1], jnp.int32),
-            pltpu.VMEM(enc_qkv.shape, BF16),
-            pltpu.SemaphoreType.DMA((4,)),
+            pltpu.VMEM((width, width), BF16),
+            pltpu.SemaphoreType.DMA((5,)),
         ],
         2_000_000_000,
         16,
@@ -341,18 +381,24 @@
         scalars=1,
         anywhere=(1, 2, 3, 4),
     )
+    mix_scratch = pltpu.VMEM((width, rows), BF16)
     (hidden_one,) = call(
         encode_kernel,
         [((rows, width), BF16)],
-        attention_scratch(3 * grid_rows, rows, width),
+        attention_scratch(3 * grid_rows, width) + [mix_scratch],
         4_000_000_000,
         16,
-        queries, pairs, counts, grid_partner, grid_off, hidden, enc_qkv, enc_out,
+        queries, pairs, counts, grid_partner, grid_off, hidden_near, pair_weights, enc_out,
     )
     one_partner = lax.ppermute(hidden_one, "nodes", inner_pairs)
-    queries, pairs = call(
+    queries, own_keys, own_kept, sums = call(
         project_kernel,
-        [((HEADS, LANES, rows), BF16), ((rows, 2 * width), BF16)],
+        [
+            ((HEADS, LANES, rows), BF16),
+            ((rows, width), BF16),
+            ((HEADS, kept_rows, rows), BF16),
+            ((HEADS, kept_rows, rows), F32),
+        ],
         [],
         1_000_000_000,
         16,
@@ -361,10 +407,10 @@
     (two_near,) = call(
         process_kernel,
         [((rows, width), BF16)],
-        attention_scratch(2 * rows, rows, width),
+        attention_scratch(rows, width) + [mix_scratch] + attention_scratch(2 * rows, width),
         4_000_000_000,
         16,
-        queries, pairs, hidden_one, one_partner, proc_qkv, proc_out,
+        queries, own_keys, own_kept, sums, hidden_one, one_partner, proc_qkv, proc_out,
     )
     two_partner, two_off = exchange(two_near)
     hidden_two, dec_queries, picked, off_picks, grid_near = call(

time: 45.5 us -> 46.2 us (1.015)
  Pallas kernels: 13.5 us -> 14.1 us
  starting transfers between devices: 24.8 us -> 25.3 us
    ppermute x1, waiting for transfers between devices: 0.72 us -> 0.01 us  [step(): one_partner = lax.ppermute(hidden_one, 'nodes', inner_pairs)]
    pallas_call x6, Pallas kernels: 13.5 us -> 14.1 us  [call(): pl.pallas_call(kernel, out_shape=[jax.ShapeDtypeStruct(shape, kind) for s...]
  transfers between devices with their start and end apart: 5 -> 5, of which waited for: 3 -> 2; matrix products, arithmetic and copies ran while one was open for 0% -> 0% of each run, Pallas kernels for 12% -> 14%
where the time goes in v4:
time: 46.2 us; the launch traced here: 46 us
  starting transfers between devices  25.3 us (55%)
  Pallas kernels  14.1 us (31%)
  waiting for transfers between devices  5.64 us (12%)
  between operations  0.79 us (2%)
    ppermute x2, starting transfers between devices, exchange(): return (lax.ppermute(shard, 'nodes', inner_pairs), off)  21.1 us
    pallas_call x6, Pallas kernels, call(): pl.pallas_call(kernel, out_shape=[jax.ShapeDtypeStruct(shape, kind) for s...  14.1 us
    ppermute x2, waiting for transfers between devices, exchange(): off = lax.ppermute(shard, 'nodes', outer_pairs)  5.63 us
    ppermute x2, starting transfers between devices, exchange(): off = lax.ppermute(shard, 'nodes', outer_pairs)  4.06 us
  transfers between devices with their start and end apart: 5, of which 2 were waited for; matrix products, arithmetic and copies ran while one was open for 0% of the time, Pallas kernels for 14%

profile of v4, /device:TPU:33, one launch (start us, length us, event | category | flops | bytes accessed | tf_op | source)
XLA Modules:
  0.0 46.0 jit_solution(7718729904170343306)
XLA Ops:
  0.6 20.5 %collective-permute-start = (bf16[128,512]{1,0:T(8,128)(2,1)}, bf16[128,512]{1,0:T(8,128)(2,1)S(1)}, u32[]{:S(2)}, u32[]{:S(2)}) collective-permute-start(bf16[128,512]{1,0:T(8,128)(2,1)} %grid_hbm.3), channel_id=1, source_target_pairs={{0,1},{1,0},{2,3},{3,2},{4,5},{5,4},{6,7},{7,6},{8,9},{9,8},{10,11... | collective-permute-start | bytes 393224 | tf_op jit(solution)/shard_map/ppermute | solution.py:359
  21.2 1.9 %collective-permute-start.1 = (bf16[128,512]{1,0:T(8,128)(2,1)}, bf16[128,512]{1,0:T(8,128)(2,1)S(1)}, u32[]{:S(2)}, u32[]{:S(2)}) collective-permute-start(bf16[128,512]{1,0:T(8,128)(2,1)} %grid_hbm.3), channel_id=1, source_target_pairs={{1,2},{3,4},{5,6},{7,8},{9,10},{11,12},{13,14},{15,16},{17,18},{19... | collective-permute-start | bytes 393224 | tf_op jit(solution)/shard_map/ppermute | solution.py:358
  23.1 0.0 copy-start.4
  23.1 2.3 %shard_map.131 = (bf16[16,128,256]{2,1,0:T(8,128)(2,1)S(1)}, bf16[128,1024]{1,0:T(8,128)(2,1)S(1)}, bf16[384,256]{1,0:T(8,128)(2,1)S(1)}, bf16[256,512]{1,0:T(8,128)(2,1)S(1)}, bf16[512,1024]{1,0:T(8,128)(2,1)S(1)}) custom-call(s32[1]{0:T(128)} %bitcast.pos_ref, bf16[128,512]{1,0:T(8,128)(2,1)} %grid_hbm.3, bf16[256,512]{1,0:T(8,128)(2,1)} %hidden_hbm.1, ...), custom_call_target="tpu_custom_call" | custom-call | flops 2000000000 | tf_op jit(solution)/shard_map/pallas_call | solution.py:324
  25.5 0.0 collective-permute-done.partner_ref
  25.5 2.2 %collective-permute-done.1.off_ref = bf16[128,512]{1,0:T(8,128)(2,1)S(1)} collective-permute-done((bf16[128,512]{1,0:T(8,128)(2,1)}, bf16[128,512]{1,0:T(8,128)(2,1)S(1)}, u32[]{:S(2)}, u32[]{:S(2)}) %collective-permute-start.1) | collective-permute-done | bytes 131104 | tf_op jit(solution)/shard_map/ppermute | solution.py:358
  27.7 2.3 %shard_map.132.hidden_ref = bf16[256,512]{1,0:T(8,128)(2,1)S(1)} custom-call(bf16[16,128,256]{2,1,0:T(8,128)(2,1)S(1)} %get-tuple-element.16.queries_ref, bf16[128,1024]{1,0:T(8,128)(2,1)S(1)} %get-tuple-element.17.pairs_ref, bf16[384,256]{1,0:T(8,128)(2,1)S(1)} %get-tuple-element.18.counts_ref, bf16[128,512]{1,0:T(8,128)(2,1)S(1)} %collective-permute-done.partner_ref, ...), custom_call_target="tpu_custom_call" | custom-call | flops 4000000000 | tf_op jit(solution)/shard_map/pallas_call | solution.py:324
  30.0 0.0 copy-start.5
  30.0 0.1 collective-permute-start.2
  30.1 2.2 %shard_map.133 = (bf16[16,128,256]{2,1,0:T(8,128)(2,1)S(1)}, bf16[256,512]{1,0:T(8,128)(2,1)S(1)}, bf16[16,48,256]{2,1,0:T(8,128)(2,1)S(1)}, f32[16,48,256]{2,1,0:T(8,128)S(1)}) custom-call(bf16[256,512]{1,0:T(8,128)(2,1)S(1)} %shard_map.132.hidden_ref, bf16[512,1536]{1,0:T(8,128)(2,1)S(1)} %copy-done.2), custom_call_target="tpu_custom_call" | custom-call | flops 1000000000 | tf_op jit(solution)/shard_map/pallas_call | solution.py:324
  32.3 0.0 collective-permute-done.2.partner_ref
  32.3 0.0 copy-start.7
  32.3 0.0 copy-start.1
  32.3 0.0 copy-start.6
  32.3 2.3 %shard_map.134.own_ref = bf16[256,512]{1,0:T(8,128)(2,1)S(1)} custom-call(bf16[16,128,256]{2,1,0:T(8,128)(2,1)S(1)} %get-tuple-element.21.queries_ref, bf16[256,512]{1,0:T(8,128)(2,1)S(1)} %get-tuple-element.22.own_keys, bf16[16,48,256]{2,1,0:T(8,128)(2,1)S(1)} %get-tuple-element.23.own_kept, f32[16,48,256]{2,1,0:T(8,128)S(1)} %get-tuple-element.24.sums_ref, ...), custom_call_target="tpu_custom_call" | custom-call | flops 4000000000 | tf_op jit(solution)/shard_map/pallas_call | solution.py:324
  34.6 0.6 %collective-permute-start.4 = (bf16[256,512]{1,0:T(8,128)(2,1)S(1)}, bf16[256,512]{1,0:T(8,128)(2,1)S(1)}, u32[]{:S(2)}, u32[]{:S(2)}) collective-permute-start(bf16[256,512]{1,0:T(8,128)(2,1)S(1)} %shard_map.134.own_ref), channel_id=1, source_target_pairs={{0,1},{1,0},{2,3},{3,2},{4,5},{5,4},{6,7},{7,6},{8,9},{9,8},{10,11... | collective-permute-start | bytes 786440 | tf_op jit(solution)/shard_map/ppermute | solution.py:359
  35.2 2.1 %collective-permute-start.3 = (bf16[256,512]{1,0:T(8,128)(2,1)S(1)}, bf16[256,512]{1,0:T(8,128)(2,1)S(1)}, u32[]{:S(2)}, u32[]{:S(2)}) collective-permute-start(bf16[256,512]{1,0:T(8,128)(2,1)S(1)} %shard_map.134.own_ref), channel_id=1, source_target_pairs={{1,2},{3,4},{5,6},{7,8},{9,10},{11,12},{13,14},{15,16},{17,18},{19... | collective-permute-start | bytes 786440 | tf_op jit(solution)/shard_map/ppermute | solution.py:358
  37.4 0.1 copy.14.nbr_ref
  37.5 0.0 copy-start.3
  37.5 0.0 collective-permute-done.4.partner_ref
  37.5 2.0 %shard_map.135 = (bf16[256,512]{1,0:T(8,128)(2,1)}, bf16[128,512]{1,0:T(8,128)(2,1)S(1)}, bf16[384,512]{1,0:T(8,128)(2,1)S(1)}, bf16[384,256]{1,0:T(8,128)(2,1)S(1)}, bf16[128,512]{1,0:T(8,128)(2,1)S(1)}) custom-call(s32[1]{0:T(128)} %bitcast.pos_ref, bf16[256,512]{1,0:T(8,128)(2,1)S(1)} %shard_map.134.own_ref, ...), custom_call_target="tpu_custom_call" | custom-call | flops 1000000000 | tf_op jit(solution)/shard_map/pallas_call | solution.py:324
  39.5 3.4 %collective-permute-done.3.off_ref = bf16[256,512]{1,0:T(8,128)(2,1)S(1)} collective-permute-done((bf16[256,512]{1,0:T(8,128)(2,1)S(1)}, bf16[256,512]{1,0:T(8,128)(2,1)S(1)}, u32[]{:S(2)}, u32[]{:S(2)}) %collective-permute-start.3) | collective-permute-done | bytes 262176 | tf_op jit(solution)/shard_map/ppermute | solution.py:358
  43.0 0.0 copy-done.6
  43.0 3.0 %shard_map.136 = bf16[128,512]{1,0:T(8,128)(2,1)} custom-call(bf16[256,512]{1,0:T(8,128)(2,1)S(1)} %collective-permute-done.3.off_ref, bf16[384,256]{1,0:T(8,128)(2,1)S(1)} %get-tuple-element.25.off_picks_ref, bf16[384,512]{1,0:T(8,128)(2,1)S(1)} %get-tuple-element.26.picked_ref, bf16[128,512]{1,0:T(8,128)(2,1)S(1)} %get-tuple-element.27.queries_ref, ...), custom_call_target="tpu_custom_call" | custom-call | flops 4000000000 | tf_op jit(solution)/shard_map/pallas_call | solution.py:324
  (9 shorter events, 0.0 us)
Async XLA Ops:
  0.6 24.8 %collective-permute-start = (bf16[128,512]{1,0:T(8,128)(2,1)}, bf16[128,512]{1,0:T(8,128)(2,1)S(1)}, u32[]{:S(2)}, u32[]{:S(2)}) collective-permute-start(bf16[128,512]{1,0:T(8,128)(2,1)} %grid_hbm.3), channel_id=1, source_target_pairs={{0,1},{1,0},{2,3},{3,2},{4,5},{5,4},{6,7},{7,6},{8,9},{9,8},{10,11... | collective-permute-start | bytes 393224 | tf_op jit(solution)/shard_map/ppermute | solution.py:359
  21.2 6.5 %collective-permute-start.1 = (bf16[128,512]{1,0:T(8,128)(2,1)}, bf16[128,512]{1,0:T(8,128)(2,1)S(1)}, u32[]{:S(2)}, u32[]{:S(2)}) collective-permute-start(bf16[128,512]{1,0:T(8,128)(2,1)} %grid_hbm.3), channel_id=1, source_target_pairs={{1,2},{3,4},{5,6},{7,8},{9,10},{11,12},{13,14},{15,16},{17,18},{19... | collective-permute-start | bytes 393224 | tf_op jit(solution)/shard_map/ppermute | solution.py:358
  23.1 4.6 %copy-start.4 = (bf16[512,512]{1,0:T(8,128)(2,1)S(1)}, bf16[512,512]{1,0:T(8,128)(2,1)}, u32[]{:S(2)}) copy-start(bf16[512,512]{1,0:T(8,128)(2,1)} %out_ref.3) | copy-start | bytes 1572868
  27.7 2.4 %copy-start.2 = (bf16[512,1536]{1,0:T(8,128)(2,1)S(1)}, bf16[512,1536]{1,0:T(8,128)(2,1)}, u32[]{:S(2)}) copy-start(bf16[512,1536]{1,0:T(8,128)(2,1)} %qkv_ref.4) | copy-start | bytes 4718596
  30.0 2.3 %copy-start.5 = (bf16[512,512]{1,0:T(8,128)(2,1)S(1)}, bf16[512,512]{1,0:T(8,128)(2,1)}, u32[]{:S(2)}) copy-start(bf16[512,512]{1,0:T(8,128)(2,1)} %out_ref.4) | copy-start | bytes 1572868
  30.0 2.3 %collective-permute-start.2 = (bf16[256,512]{1,0:T(8,128)(2,1)S(1)}, bf16[256,512]{1,0:T(8,128)(2,1)S(1)}, u32[]{:S(2)}, u32[]{:S(2)}) collective-permute-start(bf16[256,512]{1,0:T(8,128)(2,1)S(1)} %shard_map.132.hidden_ref), channel_id=1, source_target_pairs={{0,1},{1,0},{2,3},{3,2},{4,5},{5,4},{6,7},{7,6},{8,9},{9,8},{10,11... | collective-permute-start | bytes 786440 | tf_op jit(solution)/shard_map/ppermute | solution.py:393
  32.3 5.1 %copy-start.7 = (s32[128,3]{0,1:T(4,128)S(1)}, s32[128,3]{0,1:T(4,128)}, u32[]{:S(2)}) copy-start(s32[128,3]{0,1:T(4,128)} %param.15) | copy-start | bytes 4612
  32.3 10.6 %copy-start.1 = (bf16[2048,512]{1,0:T(8,128)(2,1)S(1)}, bf16[2048,512]{1,0:T(8,128)(2,1)}, u32[]{:S(2)}) copy-start(bf16[2048,512]{1,0:T(8,128)(2,1)} %mlp_out_ref.1) | copy-start | bytes 6291460
  32.3 10.6 %copy-start.6 = (bf16[512,512]{1,0:T(8,128)(2,1)S(1)}, bf16[512,512]{1,0:T(8,128)(2,1)}, u32[]{:S(2)}) copy-start(bf16[512,512]{1,0:T(8,128)(2,1)} %out_ref.5) | copy-start | bytes 1572868
  34.6 2.9 %collective-permute-start.4 = (bf16[256,512]{1,0:T(8,128)(2,1)S(1)}, bf16[256,512]{1,0:T(8,128)(2,1)S(1)}, u32[]{:S(2)}, u32[]{:S(2)}) collective-permute-start(bf16[256,512]{1,0:T(8,128)(2,1)S(1)} %shard_map.134.own_ref), channel_id=1, source_target_pairs={{0,1},{1,0},{2,3},{3,2},{4,5},{5,4},{6,7},{7,6},{8,9},{9,8},{10,11... | collective-permute-start | bytes 786440 | tf_op jit(solution)/shard_map/ppermute | solution.py:359
  35.2 7.7 %collective-permute-start.3 = (bf16[256,512]{1,0:T(8,128)(2,1)S(1)}, bf16[256,512]{1,0:T(8,128)(2,1)S(1)}, u32[]{:S(2)}, u32[]{:S(2)}) collective-permute-start(bf16[256,512]{1,0:T(8,128)(2,1)S(1)} %shard_map.134.own_ref), channel_id=1, source_target_pairs={{1,2},{3,4},{5,6},{7,8},{9,10},{11,12},{13,14},{15,16},{17,18},{19... | collective-permute-start | bytes 786440 | tf_op jit(solution)/shard_map/ppermute | solution.py:358
  37.5 5.5 %copy-start = (bf16[512,2048]{1,0:T(8,128)(2,1)S(1)}, bf16[512,2048]{1,0:T(8,128)(2,1)}, u32[]{:S(2)}) copy-start(bf16[512,2048]{1,0:T(8,128)(2,1)} %mlp_in_ref.1) | copy-start | bytes 6291460
  37.5 5.5 %copy-start.3 = (bf16[512,1536]{1,0:T(8,128)(2,1)S(1)}, bf16[512,1536]{1,0:T(8,128)(2,1)}, u32[]{:S(2)}) copy-start(bf16[512,1536]{1,0:T(8,128)(2,1)} %qkv_ref.5) | copy-start | bytes 4718596

commit v5 on v4

--- a/solution.py
+++ b/solution.py
@@ -1,5 +1,3 @@
-import functools
-
 import jax
 import jax.numpy as jnp
 from jax import lax
@@ -10,7 +8,6 @@
 HEADS = 16
 LANES = 128
 ONES = 16
-CHUNK = 256
 DEPTH = 2
 EPSILON = 1e-05
 LOG2E = 1.4426950408889634
@@ -44,33 +41,29 @@
     return inside + jnp.where(block < 0, 2, block) * rows
 
 
-def keep_values(kept, values, first):
+def keep_values(kept, values):
     head_size = values.shape[1] // HEADS
-    count = values.shape[0]
     turned = values.T
     for h in range(HEADS):
-        kept[h, :head_size, first : first + count] = turned[h * head_size : (h + 1) * head_size]
-        kept[h, head_size:, first : first + count] = jnp.ones((ONES, count), BF16)
-
-
-def weigh(q_ref, k_ref, kept, consume, counts_ref=None):
-    width = k_ref.shape[1]
-    head_size = width // HEADS
-    keys = k_ref.shape[0]
-    chunks = [slice(c, min(c + CHUNK, keys)) for c in range(0, keys, CHUNK)]
+        kept[h, :head_size] = turned[h * head_size : (h + 1) * head_size]
+        kept[h, head_size:] = jnp.ones((ONES, values.shape[0]), BF16)
+
+
+def weigh(q_ref, parts, consume):
+    head_size = parts[0][0].shape[1] // HEADS
     waiting = []
     for head in range(HEADS + DEPTH):
         scores, mixed = [], None
         tile = head * head_size // LANES * LANES
         ready = waiting.pop(0) if head >= DEPTH else None
-        for i, chunk in enumerate(chunks):
+        for i, (keys, kept, counts) in enumerate(parts):
             if head < HEADS:
-                scores.append(dot(k_ref[chunk, tile : tile + LANES], q_ref[head]))
+                scores.append(dot(keys[:, tile : tile + LANES], q_ref[head]))
             if ready is not None:
                 weights = jnp.exp2(ready[i]).astype(BF16)
-                if counts_ref is not None:
-                    weights = weights * counts_ref[chunk]
-                part = dot(kept[head - DEPTH, :, chunk], weights)
+                if counts is not None:
+                    weights = weights * counts[...]
+                part = dot(kept[head - DEPTH], weights)
                 mixed = part if mixed is None else mixed + part
         if head < HEADS:
             waiting.append(scores)
@@ -100,14 +93,17 @@
 
 
 def attend_and_add(
-    q_ref, k_ref, kept, mix, base_ref, out_ref, result_ref, exactly, counts_ref=None, sums_ref=None
-):
-    head_size = k_ref.shape[1] // HEADS
+    q_ref, own, far, mix, all_keys, all_kept, base_ref, out_ref, result_ref, counts_ref=None
+):
+    width = all_keys.shape[1]
+    head_size = width // HEADS
+    rows = own[0].shape[0]
+    counts = [None, None]
+    if counts_ref is not None:
+        counts = [counts_ref.at[:rows], counts_ref.at[rows:]]
     totals = []
 
     def consume(head, mixed):
-        if sums_ref is not None:
-            mixed = mixed + sums_ref[head]
         total = mixed[head_size : head_size + 1]
         totals.append(total)
         mix[head * head_size : (head + 1) * head_size] = (mixed[:head_size] / total).astype(BF16)
@@ -116,7 +112,7 @@
         added = dot(mix[...].T, out_ref[...])
         result_ref[...] = (base_ref[...].astype(F32) + added).astype(BF16)
 
-    weigh(q_ref, k_ref, kept, consume, counts_ref)
+    weigh(q_ref, [(*own, counts[0]), (*far, counts[1])], consume)
     least = largest = totals[0]
     for total in totals[1:]:
         least, largest = jnp.minimum(least, total), jnp.maximum(largest, total)
@@ -125,7 +121,11 @@
 
     @pl.when(jnp.logical_not(jnp.logical_and(least >= TINY, largest <= HUGE)))
     def _():
-        exactly()
+        all_keys[:rows] = own[0][...]
+        all_keys[rows:] = far[0][...]
+        all_kept[:, :, :rows] = own[1][...]
+        all_kept[:, :, rows:] = far[1][...]
+        attend_exactly(q_ref, all_keys, all_kept, mix, counts_ref)
         finish()
 
 
@@ -144,7 +144,7 @@
 
 def prepare_kernel(
     pos_ref, grid_hbm, hidden_hbm, enc_nbr_hbm, enc_qkv_hbm,
-    queries_ref, pairs_ref, counts_ref, hidden_ref, pair_weights,
+    queries_ref, keys, kept, counts_ref, hidden_ref, pair_weights,
     grid_ref, enc_nbr_ref, query_weights, arrived,
 ):
     width = grid_ref.shape[1]
@@ -182,28 +182,27 @@
         copy.wait()
     queries = dot(layer_norm(hidden_ref[...]), query_weights[...])
     spread_queries(queries_ref, (queries * scale).astype(BF16))
-    pairs_ref[...] = dot(layer_norm(grid_ref[...]), pair_weights[...]).astype(BF16)
+    pairs = dot(layer_norm(grid_ref[...]), pair_weights[...]).astype(BF16)
+    keys[...] = pairs[:, :width]
+    keep_values(kept, pairs[:, width:])
 
 
 def encode_kernel(
-    queries_ref, pairs_ref, counts_ref, partner_ref, off_ref, hidden_ref, pair_weights, out_ref,
-    result_ref, keys, kept, mix,
+    queries_ref, own_keys, own_kept, counts_ref, partner_ref, off_ref, hidden_ref, pair_weights,
+    out_ref, result_ref, keys, kept, mix, all_keys, all_kept,
 ):
     width = hidden_ref.shape[1]
-    rows = pairs_ref.shape[0]
-    keys[:rows] = pairs_ref[:, :width]
-    keep_values(kept, pairs_ref[:, width:], 0)
     normed = jnp.concatenate([layer_norm(partner_ref[...]), layer_norm(off_ref[...])], axis=0)
     pairs = dot(normed, pair_weights[...]).astype(BF16)
-    keys[rows:] = pairs[:, :width]
-    keep_values(kept, pairs[:, width:], rows)
-    exactly = functools.partial(attend_exactly, queries_ref, keys, kept, mix, counts_ref)
+    keys[...] = pairs[:, :width]
+    keep_values(kept, pairs[:, width:])
     attend_and_add(
-        queries_ref, keys, kept, mix, hidden_ref, out_ref, result_ref, exactly, counts_ref
-    )
-
-
-def project_kernel(hidden_ref, qkv_ref, queries_ref, keys, kept, sums_ref):
+        queries_ref, (own_keys, own_kept), (keys, kept), mix, all_keys, all_kept,
+        hidden_ref, out_ref, result_ref, counts_ref,
+    )
+
+
+def project_kernel(hidden_ref, qkv_ref, queries_ref, keys, kept):
     width = hidden_ref.shape[1]
     scale = LOG2E / (width // HEADS) ** 0.5
     clear_queries(queries_ref)
@@ -211,33 +210,20 @@
     spread_queries(queries_ref, (dot(normed, qkv_ref[:, :width]) * scale).astype(BF16))
     pairs = dot(normed, qkv_ref[:, width:]).astype(BF16)
     keys[...] = pairs[:, :width]
-    keep_values(kept, pairs[:, width:], 0)
-
-    def consume(head, mixed):
-        sums_ref[head] = mixed
-
-    weigh(queries_ref, keys, kept, consume)
+    keep_values(kept, pairs[:, width:])
 
 
 def process_kernel(
-    queries_ref, own_keys, own_kept, sums_ref, hidden_ref, partner_ref, qkv_ref, out_ref,
+    queries_ref, own_keys, own_kept, hidden_ref, partner_ref, qkv_ref, out_ref,
     result_ref, keys, kept, mix, all_keys, all_kept,
 ):
     width = hidden_ref.shape[1]
-    rows = hidden_ref.shape[0]
     pairs = dot(layer_norm(partner_ref[...]), qkv_ref[:, width:]).astype(BF16)
     keys[...] = pairs[:, :width]
-    keep_values(kept, pairs[:, width:], 0)
-
-    def exactly():
-        all_keys[:rows] = own_keys[...]
-        all_keys[rows:] = keys[...]
-        all_kept[:, :, :rows] = own_kept[...]
-        all_kept[:, :, rows:] = kept[...]
-        attend_exactly(queries_ref, all_keys, all_kept, mix)
-
+    keep_values(kept, pairs[:, width:])
     attend_and_add(
-        queries_ref, keys, kept, mix, hidden_ref, out_ref, result_ref, exactly, sums_ref=sums_ref
+        queries_ref, (own_keys, own_kept), (keys, kept), mix, all_keys, all_kept,
+        hidden_ref, out_ref, result_ref,
     )
 
 
@@ -360,11 +346,12 @@
 
     grid_partner, grid_off = exchange(grid)
     kept_rows = width // HEADS + ONES
-    queries, pairs, counts, hidden_near, pair_weights = call(
+    queries, own_keys, own_kept, counts, hidden_near, pair_weights = call(
         prepare_kernel,
         [
             ((HEADS, LANES, rows), BF16),
-            ((grid_rows, 2 * width), BF16),
+            ((grid_rows, width), BF16),
+            ((HEADS, kept_rows, grid_rows), BF16),
             ((3 * grid_rows, rows), BF16),
             ((rows, width), BF16),
             ((width, 2 * width), BF16),
@@ -385,19 +372,21 @@
     (hidden_one,) = call(
         encode_kernel,
         [((rows, width), BF16)],
-        attention_scratch(3 * grid_rows, width) + [mix_scratch],
+        attention_scratch(2 * grid_rows, width)
+        + [mix_scratch]
+        + attention_scratch(3 * grid_rows, width),
         4_000_000_000,
         16,
-        queries, pairs, counts, grid_partner, grid_off, hidden_near, pair_weights, enc_out,
+        queries, own_keys, own_kept, counts, grid_partner, grid_off, hidden_near, pair_weights,
+        enc_out,
     )
     one_partner = lax.ppermute(hidden_one, "nodes", inner_pairs)
-    queries, own_keys, own_kept, sums = call(
+    queries, own_keys, own_kept = call(
         project_kernel,
         [
             ((HEADS, LANES, rows), BF16),
             ((rows, width), BF16),
             ((HEADS, kept_rows, rows), BF16),
-            ((HEADS, kept_rows, rows), F32),
         ],
         [],
         1_000_000_000,
@@ -410,7 +399,7 @@
         attention_scratch(rows, width) + [mix_scratch] + attention_scratch(2 * rows, width),
         4_000_000_000,
         16,
-        queries, own_keys, own_kept, sums, hidden_one, one_partner, proc_qkv, proc_out,
+        queries, own_keys, own_kept, hidden_one, one_partner, proc_qkv, proc_out,
     )
     two_partner, two_off = exchange(two_near)
     hidden_two, dec_queries, picked, off_picks, grid_near = call(

time: 46.2 us -> 45.3 us (0.981)
  Pallas kernels: 14.1 us -> 13 us
  waiting for transfers between devices: 5.64 us -> 6.4 us
  starting transfers between devices: 25.3 us -> 24.8 us
    pallas_call x6, Pallas kernels: 14.1 us -> 13 us  [call(): pl.pallas_call(kernel, out_shape=[jax.ShapeDtypeStruct(shape, kind) for s...]
    ppermute x1, waiting for transfers between devices: 0.01 us -> 0.66 us  [step(): one_partner = lax.ppermute(hidden_one, 'nodes', inner_pairs)]
  transfers between devices with their start and end apart: 5 -> 5, of which waited for: 2 -> 3; matrix products, arithmetic and copies ran while one was open for 0% -> 0% of each run, Pallas kernels for 14% -> 12%
where the time goes in v5:
time: 45.3 us; the launch traced here: 45.1 us
  starting transfers between devices  24.8 us (55%)
  Pallas kernels  13 us (29%)
  waiting for transfers between devices  6.4 us (14%)
  between operations  0.77 us (2%)
    ppermute x2, starting transfers between devices, exchange(): return (lax.ppermute(shard, 'nodes', inner_pairs), off)  20.8 us
    pallas_call x6, Pallas kernels, call(): pl.pallas_call(kernel, out_shape=[jax.ShapeDtypeStruct(shape, kind) for s...  13 us
    ppermute x2, waiting for transfers between devices, exchange(): off = lax.ppermute(shard, 'nodes', outer_pairs)  5.74 us
    ppermute x2, starting transfers between devices, exchange(): off = lax.ppermute(shard, 'nodes', outer_pairs)  3.88 us
  transfers between devices with their start and end apart: 5, of which 3 were waited for; matrix products, arithmetic and copies ran while one was open for 0% of the time, Pallas kernels for 12%

profile of v5, /device:TPU:33, one launch (start us, length us, event | category | flops | bytes accessed | tf_op | source)
XLA Modules:
  0.0 45.1 jit_solution(14781800661101928653)
XLA Ops:
  0.6 20.5 %collective-permute-start = (bf16[128,512]{1,0:T(8,128)(2,1)}, bf16[128,512]{1,0:T(8,128)(2,1)S(1)}, u32[]{:S(2)}, u32[]{:S(2)}) collective-permute-start(bf16[128,512]{1,0:T(8,128)(2,1)} %grid_hbm.3), channel_id=1, source_target_pairs={{0,1},{1,0},{2,3},{3,2},{4,5},{5,4},{6,7},{7,6},{8,9},{9,8},{10,11... | collective-permute-start | bytes 393224 | tf_op jit(solution)/shard_map/ppermute | solution.py:345
  21.2 1.9 %collective-permute-start.1 = (bf16[128,512]{1,0:T(8,128)(2,1)}, bf16[128,512]{1,0:T(8,128)(2,1)S(1)}, u32[]{:S(2)}, u32[]{:S(2)}) collective-permute-start(bf16[128,512]{1,0:T(8,128)(2,1)} %grid_hbm.3), channel_id=1, source_target_pairs={{1,2},{3,4},{5,6},{7,8},{9,10},{11,12},{13,14},{15,16},{17,18},{19... | collective-permute-start | bytes 393224 | tf_op jit(solution)/shard_map/ppermute | solution.py:344
  23.1 0.0 copy-start.4
  23.1 2.4 %shard_map.131 = (bf16[16,128,256]{2,1,0:T(8,128)(2,1)S(1)}, bf16[128,512]{1,0:T(8,128)(2,1)S(1)}, bf16[16,48,128]{2,1,0:T(8,128)(2,1)S(1)}, bf16[384,256]{1,0:T...) custom-call(s32[1]{0:T(128)} %bitcast.pos_ref, bf16[128,512]{1,0:T(8,128)(2,1)} %grid_hbm.3, ...), custom_call_target="tpu_custom_call" | custom-call | flops 2000000000 | tf_op jit(solution)/shard_map/pallas_call | solution.py:310
  25.5 0.0 collective-permute-done.partner_ref
  25.5 2.1 %collective-permute-done.1.off_ref = bf16[128,512]{1,0:T(8,128)(2,1)S(1)} collective-permute-done((bf16[128,512]{1,0:T(8,128)(2,1)}, bf16[128,512]{1,0:T(8,128)(2,1)S(1)}, u32[]{:S(2)}, u32[]{:S(2)}) %collective-permute-start.1) | collective-permute-done | bytes 131104 | tf_op jit(solution)/shard_map/ppermute | solution.py:344
  27.7 0.0 copy-done.4
  27.7 2.2 %shard_map.132.hidden_ref = bf16[256,512]{1,0:T(8,128)(2,1)S(1)} custom-call(bf16[16,128,256]{2,1,0:T(8,128)(2,1)S(1)} %get-tuple-element.16.queries_ref, bf16[128,512]{1,0:T(8,128)(2,1)S(1)} %get-tuple-element.17.own_keys, bf16[16,48,128]{2,1,0:T(8,128)(2,1)S(1)} %get-tuple-element.18.own_kept, bf16[384,256]{1,0:T(8,128)(2,1)S(1)} %get-tuple-element.19.counts_ref, ...), custom_call_target="tpu_custom_call" | custom-call | flops 4000000000 | tf_op jit(solution)/shard_map/pallas_call | solution.py:310
  29.9 0.0 copy-start.5
  29.9 0.1 collective-permute-start.2
  30.0 0.0 copy-done.2
  30.0 0.8 %shard_map.133 = (bf16[16,128,256]{2,1,0:T(8,128)(2,1)S(1)}, bf16[256,512]{1,0:T(8,128)(2,1)S(1)}, bf16[16,48,256]{2,1,0:T(8,128)(2,1)S(1)}) custom-call(bf16[256,512]{1,0:T(8,128)(2,1)S(1)} %shard_map.132.hidden_ref, bf16[512,1536]{1,0:T(8,128)(2,1)S(1)} %copy-done.2), custom_call_target="tpu_custom_call" | custom-call | flops 1000000000 | tf_op jit(solution)/shard_map/pallas_call | solution.py:310
  30.9 0.7 %collective-permute-done.2.partner_ref = bf16[256,512]{1,0:T(8,128)(2,1)S(1)} collective-permute-done((bf16[256,512]{1,0:T(8,128)(2,1)S(1)}, bf16[256,512]{1,0:T(8,128)(2,1)S(1)}, u32[]{:S(2)}, u32[]{:S(2)}) %collective-permute-start.2) | collective-permute-done | bytes 262176 | tf_op jit(solution)/shard_map/ppermute | solution.py:383
  31.5 0.0 copy-done.5
  31.5 2.5 %shard_map.134.own_ref = bf16[256,512]{1,0:T(8,128)(2,1)S(1)} custom-call(bf16[16,128,256]{2,1,0:T(8,128)(2,1)S(1)} %get-tuple-element.22.queries_ref, bf16[256,512]{1,0:T(8,128)(2,1)S(1)} %get-tuple-element.23.own_keys, bf16[16,48,256]{2,1,0:T(8,128)(2,1)S(1)} %get-tuple-element.24.own_kept, bf16[256,512]{1,0:T(8,128)(2,1)S(1)} %shard_map.132.hidden_ref, ...), custom_call_target="tpu_custom_call" | custom-call | flops 4000000000 | tf_op jit(solution)/shard_map/pallas_call | solution.py:310
  34.1 0.3 collective-permute-start.4
  34.3 1.9 %collective-permute-start.3 = (bf16[256,512]{1,0:T(8,128)(2,1)S(1)}, bf16[256,512]{1,0:T(8,128)(2,1)S(1)}, u32[]{:S(2)}, u32[]{:S(2)}) collective-permute-start(bf16[256,512]{1,0:T(8,128)(2,1)S(1)} %shard_map.134.own_ref), channel_id=1, source_target_pairs={{1,2},{3,4},{5,6},{7,8},{9,10},{11,12},{13,14},{15,16},{17,18},{19... | collective-permute-start | bytes 786440 | tf_op jit(solution)/shard_map/ppermute | solution.py:344
  36.3 0.1 copy.14.nbr_ref
  36.4 0.0 copy-start.3
  36.4 0.0 collective-permute-done.4.partner_ref
  36.4 2.0 %shard_map.135 = (bf16[256,512]{1,0:T(8,128)(2,1)}, bf16[128,512]{1,0:T(8,128)(2,1)S(1)}, bf16[384,512]{1,0:T(8,128)(2,1)S(1)}, bf16[384,256]{1,0:T(8,128)(2,1)S(1)}, bf16[128,512]{1,0:T(8,128)(2,1)S(1)}) custom-call(s32[1]{0:T(128)} %bitcast.pos_ref, bf16[256,512]{1,0:T(8,128)(2,1)S(1)} %shard_map.134.own_ref, ...), custom_call_target="tpu_custom_call" | custom-call | flops 1000000000 | tf_op jit(solution)/shard_map/pallas_call | solution.py:310
  38.4 3.6 %collective-permute-done.3.off_ref = bf16[256,512]{1,0:T(8,128)(2,1)S(1)} collective-permute-done((bf16[256,512]{1,0:T(8,128)(2,1)S(1)}, bf16[256,512]{1,0:T(8,128)(2,1)S(1)}, u32[]{:S(2)}, u32[]{:S(2)}) %collective-permute-start.3) | collective-permute-done | bytes 262176 | tf_op jit(solution)/shard_map/ppermute | solution.py:344
  42.0 0.0 copy-done.3
  42.1 3.0 %shard_map.136 = bf16[128,512]{1,0:T(8,128)(2,1)} custom-call(bf16[256,512]{1,0:T(8,128)(2,1)S(1)} %collective-permute-done.3.off_ref, bf16[384,256]{1,0:T(8,128)(2,1)S(1)} %get-tuple-element.25.off_picks_ref, bf16[384,512]{1,0:T(8,128)(2,1)S(1)} %get-tuple-element.26.picked_ref, bf16[128,512]{1,0:T(8,128)(2,1)S(1)} %get-tuple-element.27.queries_ref, ...), custom_call_target="tpu_custom_call" | custom-call | flops 4000000000 | tf_op jit(solution)/shard_map/pallas_call | solution.py:310
  (9 shorter events, 0.0 us)
Async XLA Ops:
  0.6 24.9 %collective-permute-start = (bf16[128,512]{1,0:T(8,128)(2,1)}, bf16[128,512]{1,0:T(8,128)(2,1)S(1)}, u32[]{:S(2)}, u32[]{:S(2)}) collective-permute-start(bf16[128,512]{1,0:T(8,128)(2,1)} %grid_hbm.3), channel_id=1, source_target_pairs={{0,1},{1,0},{2,3},{3,2},{4,5},{5,4},{6,7},{7,6},{8,9},{9,8},{10,11... | collective-permute-start | bytes 393224 | tf_op jit(solution)/shard_map/ppermute | solution.py:345
  21.2 6.5 %collective-permute-start.1 = (bf16[128,512]{1,0:T(8,128)(2,1)}, bf16[128,512]{1,0:T(8,128)(2,1)S(1)}, u32[]{:S(2)}, u32[]{:S(2)}) collective-permute-start(bf16[128,512]{1,0:T(8,128)(2,1)} %grid_hbm.3), channel_id=1, source_target_pairs={{1,2},{3,4},{5,6},{7,8},{9,10},{11,12},{13,14},{15,16},{17,18},{19... | collective-permute-start | bytes 393224 | tf_op jit(solution)/shard_map/ppermute | solution.py:344
  23.1 4.6 %copy-start.4 = (bf16[512,512]{1,0:T(8,128)(2,1)S(1)}, bf16[512,512]{1,0:T(8,128)(2,1)}, u32[]{:S(2)}) copy-start(bf16[512,512]{1,0:T(8,128)(2,1)} %out_ref.3) | copy-start | bytes 1572868
  27.7 2.3 %copy-start.2 = (bf16[512,1536]{1,0:T(8,128)(2,1)S(1)}, bf16[512,1536]{1,0:T(8,128)(2,1)}, u32[]{:S(2)}) copy-start(bf16[512,1536]{1,0:T(8,128)(2,1)} %qkv_ref.4) | copy-start | bytes 4718596
  29.9 1.7 %copy-start.5 = (bf16[512,512]{1,0:T(8,128)(2,1)S(1)}, bf16[512,512]{1,0:T(8,128)(2,1)}, u32[]{:S(2)}) copy-start(bf16[512,512]{1,0:T(8,128)(2,1)} %out_ref.4) | copy-start | bytes 1572868
  29.9 1.7 %collective-permute-start.2 = (bf16[256,512]{1,0:T(8,128)(2,1)S(1)}, bf16[256,512]{1,0:T(8,128)(2,1)S(1)}, u32[]{:S(2)}, u32[]{:S(2)}) collective-permute-start(bf16[256,512]{1,0:T(8,128)(2,1)S(1)} %shard_map.132.hidden_ref), channel_id=1, source_target_pairs={{0,1},{1,0},{2,3},{3,2},{4,5},{5,4},{6,7},{7,6},{8,9},{9,8},{10,11... | collective-permute-start | bytes 786440 | tf_op jit(solution)/shard_map/ppermute | solution.py:383
  31.5 4.8 %copy-start.7 = (s32[128,3]{0,1:T(4,128)S(1)}, s32[128,3]{0,1:T(4,128)}, u32[]{:S(2)}) copy-start(s32[128,3]{0,1:T(4,128)} %param.15) | copy-start | bytes 4612
  31.5 10.5 %copy-start.1 = (bf16[2048,512]{1,0:T(8,128)(2,1)S(1)}, bf16[2048,512]{1,0:T(8,128)(2,1)}, u32[]{:S(2)}) copy-start(bf16[2048,512]{1,0:T(8,128)(2,1)} %mlp_out_ref.1) | copy-start | bytes 6291460
  31.5 10.5 %copy-start.6 = (bf16[512,512]{1,0:T(8,128)(2,1)S(1)}, bf16[512,512]{1,0:T(8,128)(2,1)}, u32[]{:S(2)}) copy-start(bf16[512,512]{1,0:T(8,128)(2,1)} %out_ref.5) | copy-start | bytes 1572868
  34.1 2.3 %collective-permute-start.4 = (bf16[256,512]{1,0:T(8,128)(2,1)S(1)}, bf16[256,512]{1,0:T(8,128)(2,1)S(1)}, u32[]{:S(2)}, u32[]{:S(2)}) collective-permute-start(bf16[256,512]{1,0:T(8,128)(2,1)S(1)} %shard_map.134.own_ref), channel_id=1, source_target_pairs={{0,1},{1,0},{2,3},{3,2},{4,5},{5,4},{6,7},{7,6},{8,9},{9,8},{10,11... | collective-permute-start | bytes 786440 | tf_op jit(solution)/shard_map/ppermute | solution.py:345
  34.3 7.7 %collective-permute-start.3 = (bf16[256,512]{1,0:T(8,128)(2,1)S(1)}, bf16[256,512]{1,0:T(8,128)(2,1)S(1)}, u32[]{:S(2)}, u32[]{:S(2)}) collective-permute-start(bf16[256,512]{1,0:T(8,128)(2,1)S(1)} %shard_map.134.own_ref), channel_id=1, source_target_pairs={{1,2},{3,4},{5,6},{7,8},{9,10},{11,12},{13,14},{15,16},{17,18},{19... | collective-permute-start | bytes 786440 | tf_op jit(solution)/shard_map/ppermute | solution.py:344
  36.4 5.6 %copy-start = (bf16[512,2048]{1,0:T(8,128)(2,1)S(1)}, bf16[512,2048]{1,0:T(8,128)(2,1)}, u32[]{:S(2)}) copy-start(bf16[512,2048]{1,0:T(8,128)(2,1)} %mlp_in_ref.1) | copy-start | bytes 6291460
  36.4 5.6 %copy-start.3 = (bf16[512,1536]{1,0:T(8,128)(2,1)S(1)}, bf16[512,1536]{1,0:T(8,128)(2,1)}, u32[]{:S(2)}) copy-start(bf16[512,1536]{1,0:T(8,128)(2,1)} %qkv_ref.5) | copy-start | bytes 4718596
